TPU v7x, 32 devices: a 4x4x1 block of a 4x4x8 slice. The times are simulated.
32 devices in a mesh: dp: 1 (over z), sp2: 4 (over y), sp: 8 (over x, core).
Axes of the slice: x: 4, y: 4, z: 1, core: 2. Of those that a mesh axis runs over, the one named last changes fastest.
The devices are a block of a 4x4x8 slice.
Arguments:
- x: bfloat16 [8, 32, 192, 512], P('dp', 'sp', 'sp2')
- w_a: bfloat16 [4, 3, 3, 512, 512], replicated
- bn_a: float32 [4, 2, 512], replicated
- w_down: bfloat16 [3, 3, 512, 1024], replicated
- bn_down: float32 [2, 1024], replicated
- w_b: bfloat16 [1, 3, 3, 1024, 1024], replicated
- bn_b: float32 [1, 2, 1024], replicated
Outputs:
- output: bfloat16 [8, 16, 96, 1024], P('dp', 'sp', 'sp2')
All inputs are finite; a program needn't handle non-finite values.
Results may differ from a plain program's by a relative error of at most 0.0108284.
Values are sent between devices in bfloat16 or wider.
A program may use at most 768 MiB of HBM per device.

v0:
```python
import jax
import jax.numpy as jnp
from jax import lax
from jax.sharding import PartitionSpec as P

CONV_DIMS = ("NHWC", "HWIO", "NHWC")


def edge_extend(act_tile, axis_name, axis_len, line_dim, two_sided):
    tile_len = act_tile.shape[line_dim]
    first_line = lax.slice_in_dim(act_tile, 0, 1, axis=line_dim)
    from_next = lax.ppermute(first_line, axis_name, perm=[(device + 1, device) for device in range(axis_len - 1)])
    if two_sided:
        last_line = lax.slice_in_dim(act_tile, tile_len - 1, tile_len, axis=line_dim)
        from_prev = lax.ppermute(last_line, axis_name, perm=[(device, device + 1) for device in range(axis_len - 1)])
        return jnp.concatenate([from_prev, act_tile, from_next], axis=line_dim)
    return jnp.concatenate([act_tile, from_next], axis=line_dim)


def conv_bn(act_tile, weight, norm_pair, stride, grid_shape):
    rows_n, cols_n = grid_shape
    two_sided = stride == 1
    extended = edge_extend(act_tile, "sp", rows_n, 1, two_sided)
    extended = edge_extend(extended, "sp2", cols_n, 2, two_sided)
    pre_norm = lax.conv_general_dilated(extended, weight, (stride, stride), "VALID", dimension_numbers=CONV_DIMS, preferred_element_type=jnp.float32)
    moments = jnp.stack([jnp.sum(pre_norm, axis=(0, 1, 2)), jnp.sum(pre_norm * pre_norm, axis=(0, 1, 2))])
    moments = lax.psum(moments, ("sp2", "sp"))
    num_pos = pre_norm.shape[0] * pre_norm.shape[1] * pre_norm.shape[2] * rows_n * cols_n
    mean_val = moments[0] / num_pos
    var_val = moments[1] / num_pos - mean_val * mean_val
    normed = norm_pair[0] * (pre_norm - mean_val) * lax.rsqrt(var_val + 1e-5) + norm_pair[1]
    return jnp.maximum(normed, 0.0).astype(jnp.bfloat16)


def solution(mesh):
    grid_shape = (mesh.shape["sp"], mesh.shape["sp2"])

    def per_device(x, w_a, bn_a, w_down, bn_down, w_b, bn_b):
        act_tile = x
        for layer_idx in range(w_a.shape[0]):
            act_tile = conv_bn(act_tile, w_a[layer_idx], bn_a[layer_idx], 1, grid_shape)
        act_tile = conv_bn(act_tile, w_down, bn_down, 2, grid_shape)
        for layer_idx in range(w_b.shape[0]):
            act_tile = conv_bn(act_tile, w_b[layer_idx], bn_b[layer_idx], 1, grid_shape)
        return act_tile

    tile_spec = P("dp", "sp", "sp2", None)
    return jax.shard_map(per_device, mesh=mesh, in_specs=(tile_spec, P(), P(), P(), P(), P(), P()), out_specs=tile_spec, check_vma=False)
```

profile of v0, /device:TPU:97, one launch (start us, length us, event | category | flops | bytes accessed | tf_op | source)
XLA Modules:
  0.0 454.3 jit_solution(15419987931152658528)
XLA Ops:
  0.0 1.3 fusion.77
  1.3 0.2 copy.13
  1.5 4.6 %collective-permute-start = (bf16[8,1,48,512]{3,0,2,1:T(8,128)(2,1)S(1)}, bf16[8,1,48,512]{3,0,2,1:T(8,128)(2,1)S(1)}, u32[]{:S(2)}, u32[]{:S(2)}) collective-permute-start(bf16[8,1,48,512]{3,0,2,1:T(8,128)(2,1)S(1)} %copy.13), channel_id=1, source_target_pairs={{0,1},{1,2},{2,3},{3,4},{4,5},{5,6},{6,7},{8,9},{9,10},{10,11},{11... | collective-permute-start | bytes 1179656 | tf_op jit(solution)/shard_map/ppermute | solution.py:15
  6.1 0.2 copy.14
  6.4 2.0 collective-permute-start.1
  8.3 2.5 collective-permute-done
  10.9 0.9 constant_dynamic-update-slice_fusion.1
  11.7 3.8 collective-permute-done.1
  15.6 4.0 collective-permute-start.2
  19.5 1.3 collective-permute-start.3
  20.9 3.9 collective-permute-done.3
  24.8 12.1 %fusion.70 = (f32[512]{0:T(512)S(1)}, f32[512]{0:T(512)S(1)}, f32[8,4,48,512]{3,0,2,1:T(8,128)S(1)}) fusion(bf16[4,3,3,512,512]{4,3,2,1,0:T(8,128)(2,1)} %param.8, bf16[8,6,1,512]{3,0,2,1:T(8,128)(2,1)S(1)} %collective-permute-done.3, bf16[8,6,48,512]{3,0,2,1:T(8,128)(2,1)S(1)} %constant_dynamic-update-slice_fusion, ...), kind=kOutput, calls=%fused_computation.122 | convolution fusion | flops 7252573184 | bytes 10326016 | tf_op jit(solution)/shard_map/conv_general_dilated | solution.py:25
  36.9 45.6 %psum.42 = f32[2,512]{1,0:T(2,128)S(1)} all-reduce(f32[2,512]{1,0:T(2,128)S(1)} %pad_maximum_fusion.15), channel_id=1, replica_groups=mesh['dp'=1,'sp2'=4,'sp'=8] {'sp2','sp'}, use_global_device_ids=true, to_apply=%region_2.0 | all-reduce | flops 1024 | bytes 8192 | tf_op jit(solution)/shard_map/psum | solution.py:27
  82.6 0.6 maximum_convert_fusion.3
  83.1 0.1 fusion.76
  83.2 2.1 collective-permute-start.4
  85.4 2.3 collective-permute-start.5
  87.6 2.4 collective-permute-done.4
  90.0 4.4 collective-permute-done.5
  94.5 2.4 collective-permute-start.6
  96.9 1.5 collective-permute-start.7
  98.4 3.4 collective-permute-done.7
  101.8 12.2 %fusion.69 = (f32[512]{0:T(512)S(1)}, f32[512]{0:T(512)S(1)}, f32[8,4,48,512]{3,0,2,1:T(8,128)S(1)}) fusion(bf16[4,3,3,512,512]{4,3,2,1,0:T(8,128)(2,1)} %param.8, bf16[8,6,1,512]{3,0,2,1:T(8,128)(2,1)S(1)} %collective-permute-done.7, bf16[8,1,48,512]{3,0,2,1:T(8,128)(2,1)S(1)} %collective-permute-done.5, ...), kind=kOutput, calls=%fused_computation.121 | convolution fusion | flops 7255030784 | bytes 10326016 | tf_op jit(solution)/shard_map/conv_general_dilated | solution.py:25
  114.0 44.9 %psum.43 = f32[2,512]{1,0:T(2,128)S(1)} all-reduce(f32[2,512]{1,0:T(2,128)S(1)} %pad_maximum_fusion.16), channel_id=1, replica_groups=mesh['dp'=1,'sp2'=4,'sp'=8] {'sp2','sp'}, use_global_device_ids=true, to_apply=%region_5.0 | all-reduce | flops 1024 | bytes 8192 | tf_op jit(solution)/shard_map/psum | solution.py:27
  158.9 0.6 maximum_convert_fusion.2
  159.5 0.1 fusion.75
  159.6 2.2 collective-permute-start.8
  161.8 2.2 collective-permute-start.9
  164.0 2.5 collective-permute-done.8
  166.5 4.4 collective-permute-done.9
  171.0 2.3 collective-permute-start.10
  173.3 1.3 collective-permute-start.11
  174.6 3.5 collective-permute-done.11
  178.2 12.2 %fusion.68 = (f32[512]{0:T(512)S(1)}, f32[512]{0:T(512)S(1)}, f32[8,4,48,512]{3,0,2,1:T(8,128)S(1)}) fusion(bf16[4,3,3,512,512]{4,3,2,1,0:T(8,128)(2,1)} %param.8, bf16[8,6,1,512]{3,0,2,1:T(8,128)(2,1)S(1)} %collective-permute-done.11, bf16[8,1,48,512]{3,0,2,1:T(8,128)(2,1)S(1)} %collective-permute-done.9, ...), kind=kOutput, calls=%fused_computation.120 | convolution fusion | flops 7255030784 | bytes 10326016 | tf_op jit(solution)/shard_map/conv_general_dilated | solution.py:25
  190.4 45.2 %psum.44 = f32[2,512]{1,0:T(2,128)S(1)} all-reduce(f32[2,512]{1,0:T(2,128)S(1)} %pad_maximum_fusion.17), channel_id=1, replica_groups=mesh['dp'=1,'sp2'=4,'sp'=8] {'sp2','sp'}, use_global_device_ids=true, to_apply=%region_8.0 | all-reduce | flops 1024 | bytes 8192 | tf_op jit(solution)/shard_map/psum | solution.py:27
  235.6 0.6 maximum_convert_fusion.1
  236.2 2.2 collective-permute-start.12
  238.5 2.2 collective-permute-start.13
  240.7 2.5 collective-permute-done.12
  243.2 4.4 collective-permute-done.13
  247.6 2.3 collective-permute-start.14
  250.0 1.3 collective-permute-start.15
  251.3 3.5 collective-permute-done.15
  254.8 12.2 %fusion.67 = (f32[512]{0:T(512)S(1)}, f32[512]{0:T(512)S(1)}, f32[8,4,48,512]{3,0,2,1:T(8,128)S(1)}) fusion(bf16[4,3,3,512,512]{4,3,2,1,0:T(8,128)(2,1)} %param.8, bf16[8,6,1,512]{3,0,2,1:T(8,128)(2,1)S(1)} %collective-permute-done.15, bf16[8,1,48,512]{3,0,2,1:T(8,128)(2,1)S(1)} %collective-permute-done.13, ...), kind=kOutput, calls=%fused_computation.119 | convolution fusion | flops 7255030784 | bytes 10326016 | tf_op jit(solution)/shard_map/conv_general_dilated | solution.py:25
  267.0 45.0 %psum.45 = f32[2,512]{1,0:T(2,128)S(1)} all-reduce(f32[2,512]{1,0:T(2,128)S(1)} %pad_maximum_fusion.18), channel_id=1, replica_groups=mesh['dp'=1,'sp2'=4,'sp'=8] {'sp2','sp'}, use_global_device_ids=true, to_apply=%region_11.0 | all-reduce | flops 1024 | bytes 8192 | tf_op jit(solution)/shard_map/psum | solution.py:27
  312.0 0.6 maximum_convert_fusion
  312.7 2.9 collective-permute-start.16
  315.6 6.2 %collective-permute-done.16 = bf16[8,1,48,512]{3,0,2,1:T(8,128)(2,1)S(1)} collective-permute-done((bf16[8,1,48,512]{3,0,2,1:T(8,128)(2,1)S(1)}, bf16[8,1,48,512]{3,0,2,1:T(8,128)(2,1)S(1)}, u32[]{:S(2)}, u32[]{:S(2)}) %collective-permute-start.16) | collective-permute-done | bytes 393248 | tf_op jit(solution)/shard_map/ppermute | solution.py:12
  321.8 1.3 collective-permute-start.17
  323.2 3.4 collective-permute-done.17
  326.6 6.4 %fusion.72 = (f32[1024]{0:T(1024)S(1)}, f32[1024]{0:T(1024)S(1)}, f32[8,2,24,1024]{3,0,2,1:T(8,128)S(1)}) fusion(bf16[3,3,512,1024]{3,2,1,0:T(8,128)(2,1)} %param.10, bf16[8,5,1,512]{3,0,2,1:T(8,128)(2,1)S(1)} %collective-permute-done.17, bf16[8,1,48,512]{3,0,2,1:T(8,128)(2,1)S(1)} %collective-permute-done.16, ...), kind=kOutput, calls=%fused_computation.124 | convolution fusion | flops 3627063296 | bytes 13025280 | tf_op jit(solution)/shard_map/conv_general_dilated | solution.py:25
  333.0 43.6 %psum.46 = f32[2,1024]{1,0:T(2,128)S(1)} all-reduce(f32[2,1024]{1,0:T(2,128)S(1)} %pad_maximum_fusion.13), channel_id=1, replica_groups=mesh['dp'=1,'sp2'=4,'sp'=8] {'sp2','sp'}, use_global_device_ids=true, to_apply=%region_14.0 | all-reduce | flops 2048 | bytes 16384 | tf_op jit(solution)/shard_map/psum | solution.py:27
  376.6 0.3 maximum_convert_fusion.5
  377.0 2.6 collective-permute-start.18
  379.6 2.0 collective-permute-start.19
  381.6 2.7 collective-permute-done.18
  384.3 4.4 collective-permute-done.19
  388.8 2.0 collective-permute-start.20
  390.8 1.3 collective-permute-start.21
  392.2 3.7 collective-permute-done.21
  395.9 11.4 %fusion.71 = (f32[1024]{0:T(1024)S(1)}, f32[1024]{0:T(1024)S(1)}, f32[8,2,24,1024]{3,0,2,1:T(8,128)S(1)}) fusion(bf16[1,3,3,1024,1024]{4,3,2,1,0:T(8,128)(2,1)} %param.12, bf16[8,4,1,1024]{3,0,2,1:T(8,128)(2,1)S(1)} %collective-permute-done.21, bf16[8,1,24,1024]{3,0,2,1:T(8,128)(2,1)S(1)} %collective-permute-done.19, ...), kind=kOutput, calls=%fused_computation.123 | convolution fusion | flops 7252342784 | bytes 22159360 | tf_op jit(solution)/shard_map/conv_general_dilated | solution.py:25
  407.3 44.9 %psum.47 = f32[2,1024]{1,0:T(2,128)S(1)} all-reduce(f32[2,1024]{1,0:T(2,128)S(1)} %pad_maximum_fusion.14), channel_id=1, replica_groups=mesh['dp'=1,'sp2'=4,'sp'=8] {'sp2','sp'}, use_global_device_ids=true, to_apply=%region_17.0 | all-reduce | flops 2048 | bytes 16384 | tf_op jit(solution)/shard_map/psum | solution.py:27
  452.3 0.3 maximum_convert_fusion.4
  452.6 1.3 copy.11
  (45 shorter events, 0.5 us)
Async XLA Ops:
  0.0 10.8 %copy-start = (bf16[8,4,48,512]{3,2,1,0:T(8,128)(2,1)S(1)}, bf16[8,4,48,512]{3,2,1,0:T(8,128)(2,1)}, u32[]{:S(2)}) copy-start(bf16[8,4,48,512]{3,2,1,0:T(8,128)(2,1)} %param.7) | copy-start | bytes 4718596
  1.5 9.3 %collective-permute-start = (bf16[8,1,48,512]{3,0,2,1:T(8,128)(2,1)S(1)}, bf16[8,1,48,512]{3,0,2,1:T(8,128)(2,1)S(1)}, u32[]{:S(2)}, u32[]{:S(2)}) collective-permute-start(bf16[8,1,48,512]{3,0,2,1:T(8,128)(2,1)S(1)} %copy.13), channel_id=1, source_target_pairs={{0,1},{1,2},{2,3},{3,4},{4,5},{5,6},{6,7},{8,9},{9,10},{10,11},{11... | collective-permute-start | bytes 1179656 | tf_op jit(solution)/shard_map/ppermute | solution.py:15
  6.4 14.5 %copy-start.1 = (f32[4,2,512]{2,1,0:T(2,128)S(1)}, f32[4,2,512]{2,1,0:T(2,128)}, u32[]{:S(2)}) copy-start(f32[4,2,512]{2,1,0:T(2,128)} %param.9) | copy-start | bytes 49156
  6.4 9.1 %collective-permute-start.1 = (bf16[8,1,48,512]{3,0,2,1:T(8,128)(2,1)S(1)}, bf16[8,1,48,512]{3,0,2,1:T(8,128)(2,1)S(1)}, u32[]{:S(2)}, u32[]{:S(2)}) collective-permute-start(bf16[8,1,48,512]{3,0,2,1:T(8,128)(2,1)S(1)} %copy.14), channel_id=1, source_target_pairs={{1,0},{2,1},{3,2},{4,3},{5,4},{6,5},{7,6},{9,8},{10,9},{11,10},{12... | collective-permute-start | bytes 1179656 | tf_op jit(solution)/shard_map/ppermute | solution.py:12
  15.6 5.3 %collective-permute-start.2 = (bf16[8,6,1,512]{3,0,2,1:T(8,128)(2,1)S(1)}, bf16[8,6,1,512]{3,0,2,1:T(8,128)(2,1)S(1)}, u32[]{:S(2)}, u32[]{:S(2)}) collective-permute-start(bf16[8,6,1,512]{3,0,2,1:T(8,128)(2,1)S(1)} %get-tuple-element.23), channel_id=1, source_target_pairs={{0,8},{8,16},{16,24},{1,9},{9,17},{17,25},{2,10},{10,18},{18,26},{... | collective-permute-start | bytes 147464 | tf_op jit(solution)/shard_map/ppermute | solution.py:15
  19.5 5.3 %collective-permute-start.3 = (bf16[8,6,1,512]{3,0,2,1:T(8,128)(2,1)S(1)}, bf16[8,6,1,512]{3,0,2,1:T(8,128)(2,1)S(1)}, u32[]{:S(2)}, u32[]{:S(2)}) collective-permute-start(bf16[8,6,1,512]{3,0,2,1:T(8,128)(2,1)S(1)} %get-tuple-element.24), channel_id=1, source_target_pairs={{8,0},{16,8},{24,16},{9,1},{17,9},{25,17},{10,2},{18,10},{26,18},{... | collective-permute-start | bytes 147464 | tf_op jit(solution)/shard_map/ppermute | solution.py:12
  83.2 6.8 %collective-permute-start.4 = (bf16[8,1,48,512]{3,0,2,1:T(8,128)(2,1)S(1)}, bf16[8,1,48,512]{3,0,2,1:T(8,128)(2,1)S(1)}, u32[]{:S(2)}, u32[]{:S(2)}) collective-permute-start(bf16[8,1,48,512]{3,0,2,1:T(8,128)(2,1)S(1)} %get-tuple-element.31), channel_id=1, source_target_pairs={{0,1},{1,2},{2,3},{3,4},{4,5},{5,6},{6,7},{8,9},{9,10},{10,11},{11... | collective-permute-start | bytes 1179656 | tf_op jit(solution)/shard_map/ppermute | solution.py:15
  85.4 9.1 %collective-permute-start.5 = (bf16[8,1,48,512]{3,0,2,1:T(8,128)(2,1)S(1)}, bf16[8,1,48,512]{3,0,2,1:T(8,128)(2,1)S(1)}, u32[]{:S(2)}, u32[]{:S(2)}) collective-permute-start(bf16[8,1,48,512]{3,0,2,1:T(8,128)(2,1)S(1)} %get-tuple-element.32), channel_id=1, source_target_pairs={{1,0},{2,1},{3,2},{4,3},{5,4},{6,5},{7,6},{9,8},{10,9},{11,10},{12... | collective-permute-start | bytes 1179656 | tf_op jit(solution)/shard_map/ppermute | solution.py:12
  94.5 3.9 collective-permute-start.6
  96.9 4.9 %collective-permute-start.7 = (bf16[8,6,1,512]{3,0,2,1:T(8,128)(2,1)S(1)}, bf16[8,6,1,512]{3,0,2,1:T(8,128)(2,1)S(1)}, u32[]{:S(2)}, u32[]{:S(2)}) collective-permute-start(bf16[8,6,1,512]{3,0,2,1:T(8,128)(2,1)S(1)} %get-tuple-element.22), channel_id=1, source_target_pairs={{8,0},{16,8},{24,16},{9,1},{17,9},{25,17},{10,2},{18,10},{26,18},{... | collective-permute-start | bytes 147464 | tf_op jit(solution)/shard_map/ppermute | solution.py:12
  159.6 6.9 %collective-permute-start.8 = (bf16[8,1,48,512]{3,0,2,1:T(8,128)(2,1)S(1)}, bf16[8,1,48,512]{3,0,2,1:T(8,128)(2,1)S(1)}, u32[]{:S(2)}, u32[]{:S(2)}) collective-permute-start(bf16[8,1,48,512]{3,0,2,1:T(8,128)(2,1)S(1)} %get-tuple-element.29), channel_id=1, source_target_pairs={{0,1},{1,2},{2,3},{3,4},{4,5},{5,6},{6,7},{8,9},{9,10},{10,11},{11... | collective-permute-start | bytes 1179656 | tf_op jit(solution)/shard_map/ppermute | solution.py:15
  161.8 9.1 %collective-permute-start.9 = (bf16[8,1,48,512]{3,0,2,1:T(8,128)(2,1)S(1)}, bf16[8,1,48,512]{3,0,2,1:T(8,128)(2,1)S(1)}, u32[]{:S(2)}, u32[]{:S(2)}) collective-permute-start(bf16[8,1,48,512]{3,0,2,1:T(8,128)(2,1)S(1)} %get-tuple-element.30), channel_id=1, source_target_pairs={{1,0},{2,1},{3,2},{4,3},{5,4},{6,5},{7,6},{9,8},{10,9},{11,10},{12... | collective-permute-start | bytes 1179656 | tf_op jit(solution)/shard_map/ppermute | solution.py:12
  171.0 3.6 collective-permute-start.10
  173.3 4.9 %collective-permute-start.11 = (bf16[8,6,1,512]{3,0,2,1:T(8,128)(2,1)S(1)}, bf16[8,6,1,512]{3,0,2,1:T(8,128)(2,1)S(1)}, u32[]{:S(2)}, u32[]{:S(2)}) collective-permute-start(bf16[8,6,1,512]{3,0,2,1:T(8,128)(2,1)S(1)} %get-tuple-element.20), channel_id=1, source_target_pairs={{8,0},{16,8},{24,16},{9,1},{17,9},{25,17},{10,2},{18,10},{26,18},{... | collective-permute-start | bytes 147464 | tf_op jit(solution)/shard_map/ppermute | solution.py:12
  236.2 6.9 %collective-permute-start.12 = (bf16[8,1,48,512]{3,0,2,1:T(8,128)(2,1)S(1)}, bf16[8,1,48,512]{3,0,2,1:T(8,128)(2,1)S(1)}, u32[]{:S(2)}, u32[]{:S(2)}) collective-permute-start(bf16[8,1,48,512]{3,0,2,1:T(8,128)(2,1)S(1)} %get-tuple-element.27), channel_id=1, source_target_pairs={{0,1},{1,2},{2,3},{3,4},{4,5},{5,6},{6,7},{8,9},{9,10},{10,11},{11... | collective-permute-start | bytes 1179656 | tf_op jit(solution)/shard_map/ppermute | solution.py:15
  238.5 9.1 %collective-permute-start.13 = (bf16[8,1,48,512]{3,0,2,1:T(8,128)(2,1)S(1)}, bf16[8,1,48,512]{3,0,2,1:T(8,128)(2,1)S(1)}, u32[]{:S(2)}, u32[]{:S(2)}) collective-permute-start(bf16[8,1,48,512]{3,0,2,1:T(8,128)(2,1)S(1)} %get-tuple-element.28), channel_id=1, source_target_pairs={{1,0},{2,1},{3,2},{4,3},{5,4},{6,5},{7,6},{9,8},{10,9},{11,10},{12... | collective-permute-start | bytes 1179656 | tf_op jit(solution)/shard_map/ppermute | solution.py:12
  247.6 3.6 collective-permute-start.14
  250.0 4.9 %collective-permute-start.15 = (bf16[8,6,1,512]{3,0,2,1:T(8,128)(2,1)S(1)}, bf16[8,6,1,512]{3,0,2,1:T(8,128)(2,1)S(1)}, u32[]{:S(2)}, u32[]{:S(2)}) collective-permute-start(bf16[8,6,1,512]{3,0,2,1:T(8,128)(2,1)S(1)} %get-tuple-element.18), channel_id=1, source_target_pairs={{8,0},{16,8},{24,16},{9,1},{17,9},{25,17},{10,2},{18,10},{26,18},{... | collective-permute-start | bytes 147464 | tf_op jit(solution)/shard_map/ppermute | solution.py:12
  312.7 10.5 %copy-start.2 = (f32[2,1024]{1,0:T(2,128)S(1)}, f32[2,1024]{1,0:T(2,128)}, u32[]{:S(2)}) copy-start(f32[2,1024]{1,0:T(2,128)} %param.11) | copy-start | bytes 24580
  312.7 9.1 %collective-permute-start.16 = (bf16[8,1,48,512]{3,0,2,1:T(8,128)(2,1)S(1)}, bf16[8,1,48,512]{3,0,2,1:T(8,128)(2,1)S(1)}, u32[]{:S(2)}, u32[]{:S(2)}) collective-permute-start(bf16[8,1,48,512]{3,0,2,1:T(8,128)(2,1)S(1)} %slice.240), channel_id=1, source_target_pairs={{1,0},{2,1},{3,2},{4,3},{5,4},{6,5},{7,6},{9,8},{10,9},{11,10},{12... | collective-permute-start | bytes 1179656 | tf_op jit(solution)/shard_map/ppermute | solution.py:12
  321.8 4.8 %collective-permute-start.17 = (bf16[8,5,1,512]{3,0,2,1:T(8,128)(2,1)S(1)}, bf16[8,5,1,512]{3,0,2,1:T(8,128)(2,1)S(1)}, u32[]{:S(2)}, u32[]{:S(2)}) collective-permute-start(bf16[8,5,1,512]{3,0,2,1:T(8,128)(2,1)S(1)} %pad_maximum_fusion.12), channel_id=1, source_target_pairs={{8,0},{16,8},{24,16},{9,1},{17,9},{25,17},{10,2},{18,10},{26,18},{... | collective-permute-start | bytes 122888 | tf_op jit(solution)/shard_map/ppermute | solution.py:12
  376.6 15.5 %copy-start.3 = (f32[1,2,1024]{2,1,0:T(2,128)S(1)}, f32[1,2,1024]{2,1,0:T(2,128)}, u32[]{:S(2)}) copy-start(f32[1,2,1024]{2,1,0:T(2,128)} %param.13) | copy-start | bytes 24580
  377.0 7.3 %collective-permute-start.18 = (bf16[8,1,24,1024]{3,0,2,1:T(8,128)(2,1)S(1)}, bf16[8,1,24,1024]{3,0,2,1:T(8,128)(2,1)S(1)}, u32[]{:S(2)}, u32[]{:S(2)}) collective-permute-start(bf16[8,1,24,1024]{3,0,2,1:T(8,128)(2,1)S(1)} %get-tuple-element.35), channel_id=1, source_target_pairs={{0,1},{1,2},{2,3},{3,4},{4,5},{5,6},{6,7},{8,9},{9,10},{10,11},{11... | collective-permute-start | bytes 1179656 | tf_op jit(solution)/shard_map/ppermute | solution.py:15
  379.6 9.1 %collective-permute-start.19 = (bf16[8,1,24,1024]{3,0,2,1:T(8,128)(2,1)S(1)}, bf16[8,1,24,1024]{3,0,2,1:T(8,128)(2,1)S(1)}, u32[]{:S(2)}, u32[]{:S(2)}) collective-permute-start(bf16[8,1,24,1024]{3,0,2,1:T(8,128)(2,1)S(1)} %get-tuple-element.36), channel_id=1, source_target_pairs={{1,0},{2,1},{3,2},{4,3},{5,4},{6,5},{7,6},{9,8},{10,9},{11,10},{12... | collective-permute-start | bytes 1179656 | tf_op jit(solution)/shard_map/ppermute | solution.py:12
  388.8 3.4 collective-permute-start.20
  390.8 5.0 %collective-permute-start.21 = (bf16[8,4,1,1024]{3,0,2,1:T(8,128)(2,1)S(1)}, bf16[8,4,1,1024]{3,0,2,1:T(8,128)(2,1)S(1)}, u32[]{:S(2)}, u32[]{:S(2)}) collective-permute-start(bf16[8,4,1,1024]{3,0,2,1:T(8,128)(2,1)S(1)} %get-tuple-element.26), channel_id=1, source_target_pairs={{8,0},{16,8},{24,16},{9,1},{17,9},{25,17},{10,2},{18,10},{26,18},{... | collective-permute-start | bytes 196616 | tf_op jit(solution)/shard_map/ppermute | solution.py:12
where the time goes:
time: 463 us; the launch traced here: 454 us
  blocking collectives  269 us (58%)
  matrix products  66.4 us (14%)
  waiting for transfers between devices  61.8 us (13%)
  starting transfers between devices  48.3 us (10%)
    psum x6, blocking collectives, conv_bn(): moments = lax.psum(moments, ('sp2', 'sp'))  269 us
    conv_general_dilated x6, matrix products, conv_bn(): lax.conv_general_dilated(extended, weight, (stride, stride), 'VALID', dim...  66.4 us
    ppermute x12, waiting for transfers between devices, edge_extend(): lax.ppermute(first_line, axis_name, perm=[(device + 1, device) for device...  49.2 us
    ppermute x10, starting transfers between devices, edge_extend(): lax.ppermute(last_line, axis_name, perm=[(device, device + 1) for device...  26.9 us
    ppermute x12, starting transfers between devices, edge_extend(): lax.ppermute(first_line, axis_name, perm=[(device + 1, device) for device...  21.4 us
    ppermute x10, waiting for transfers between devices, edge_extend(): lax.ppermute(last_line, axis_name, perm=[(device, device + 1) for device...  12.6 us
  transfers between devices with their start and end apart: 22, of which 17 were waited for; matrix products, arithmetic and copies ran while one was open for 0% of the time, Pallas kernels for 0%

commit v1 on v0

v1 whole, which is shorter than its diff:
```python
import functools

import jax
import jax.numpy as jnp
from jax import lax
from jax.experimental import pallas as pl
from jax.experimental.pallas import tpu as pltpu
from jax.sharding import PartitionSpec as P

MESH = pl.DeviceIdType.MESH
F32 = jnp.float32
BF16 = jnp.bfloat16
LANES = 128
SUB = 8
EPS = 1e-5
KINDS = ((-1, 0), (1, 0), (0, -1), (0, 1), (-1, -1), (-1, 1), (1, -1), (1, 1))


def stack_kernel(dims, x_hbm, wa_hbm, bna_ref, wd_hbm, bnd_ref, wb_hbm, bnb_ref, out_ref,
                 wsl, xs, xrow, ya, yb, za, zd, zb, rowa, rowb, csa, cra, csb, crb, sta, std, stb, acc, prm,
                 wsem, xsem, xss, xrs, hs, hr, ss, sr):
    n_i, n_j, imgs, rows, cols, chan = dims
    n_dev = n_i * n_j
    cba = chan // LANES
    cbb = 2 * cba
    pa, pb = ya.shape[3], yb.shape[3]
    ma, colb, rowsb = imgs * cols, cols // 2, rows // 2
    mb = imgs * colb
    layers_a = wa_hbm.shape[0]
    i = lax.axis_index("sp")
    j = lax.axis_index("sp2")
    me = i * n_j + j
    core = lax.rem(i, 2)
    row_loc = (rows - 1) * (1 - core)
    row_rem = (rows - 1) * core

    def here(di, dj):
        a, b = i + di, j + dj
        return (a >= 0) & (a < n_i) & (b >= 0) & (b < n_j)

    def w_copies(slot, src):
        return pltpu.make_async_copy(src, wsl.at[slot % 6], wsem.at[slot])

    def wa_copy(l):
        return w_copies(l, wa_hbm.at[l])

    def wd_copy(nh):
        return w_copies(layers_a + nh, wd_hbm.at[:, :, :, pl.ds(nh * chan, chan)])

    def wb_copy(q):
        src = wb_hbm.at[0, :, :, pl.ds((q // 2) * chan, chan), pl.ds((q % 2) * chan, chan)]
        return w_copies(layers_a + 2 + q, src)

    xcopy = pltpu.make_async_copy(x_hbm, xs, xsem)
    xcopy.start()
    for l in range(layers_a):
        wa_copy(l).start()
    for nh in range(2):
        wd_copy(nh).start()

    barrier = pltpu.get_barrier_semaphore()

    def peer(p):
        t = lax.rem(me + p, n_dev)
        return {"sp": t // n_j, "sp2": lax.rem(t, n_j)}

    def greet(p, c):
        pl.semaphore_signal(barrier, inc=1, device_id=peer(p), device_id_type=MESH)
        return c

    lax.fori_loop(1, n_dev, greet, 0)

    def wipe(y):
        def go(t, c):
            y[t] = jnp.zeros(y.shape[1:], F32)
            return c

        lax.fori_loop(0, y.shape[0], go, 0)

    wipe(ya)
    wipe(yb)

    xcopy.wait()
    pl.semaphore_wait(barrier, n_dev - 1)

    def target(k):
        di, dj = KINDS[k]
        return {"sp": i + di, "sp2": j + dj}

    def halo_copy(k, set_, z, row, cs, cr, n_rows):
        di, dj = KINDS[k]
        slot = {-1: n_rows + 1, 1: 0}.get(di)
        edge = 0 if di < 0 else n_rows - 1
        side_here, side_there = (0, 1) if dj < 0 else (1, 0)
        if dj == 0:
            src, dst = z.at[edge], row.at[1 if di < 0 else 0]
        elif di == 0:
            src, dst = cs.at[side_here], cr.at[side_there, pl.ds(1, n_rows)]
        else:
            src, dst = cs.at[side_here, edge], cr.at[side_there, slot]
        return pltpu.make_async_remote_copy(src_ref=src, dst_ref=dst, send_sem=hs.at[set_, k], recv_sem=hr.at[set_, k],
                                            device_id=target(k), device_id_type=MESH)

    def halo_start(k, *args):
        @pl.when(here(*KINDS[k]))
        def _():
            halo_copy(k, *args).start()

    def halo_sent(k, *args):
        @pl.when(here(*KINDS[k]))
        def _():
            halo_copy(k, *args).wait_send()

    def got(k):
        return here(-KINDS[k][0], -KINDS[k][1])

    def xrow_copy(k):
        di = KINDS[k][0]
        return pltpu.make_async_remote_copy(src_ref=xs.at[:, 0 if di < 0 else rows - 1], dst_ref=xrow.at[1 if di < 0 else 0],
                                            send_sem=xss.at[k], recv_sem=xrs.at[k], device_id=target(k), device_id_type=MESH)

    for k in (0, 1):
        @pl.when(here(*KINDS[k]))
        def _():
            xrow_copy(k).start()

    def lines(y):
        return y.reshape(y.shape[0], y.shape[1], y.shape[2] * y.shape[3], LANES)

    def fill_x(s, piece):
        for cb in range(cba):
            ya[s, cb, :, pl.ds(SUB, cols), :] = piece(pl.ds(cb * LANES, LANES)).astype(F32)

    def own_x(r, c):
        fill_x(r + 1, lambda cl: xs[:, r, :, cl])
        for cb in range(cba):
            csa[0, r, cb] = lines(ya)[r + 1, cb, pl.ds(SUB, imgs, stride=pa), :]
            csa[1, r, cb] = lines(ya)[r + 1, cb, pl.ds(SUB + cols - 1, imgs, stride=pa), :]
        return c

    lax.fori_loop(0, rows, own_x, 0)
    args_x = (1, za, None, csa, cra.at[1], rows)
    for k in range(2, 8):
        halo_start(k, *args_x)

    def norm(v, cb):
        mean, rs, gain, shift = (prm[q, pl.ds(cb, 1), :] for q in range(4))
        return jnp.maximum(gain * (v - mean) * rs + shift, 0.0)

    def params(st, n_pos, bn, n_cb):
        tot = st[0]
        for d in range(1, n_dev):
            tot = tot + st[d]
        mean = tot[0:n_cb] / n_pos
        var = tot[n_cb:2 * n_cb] / n_pos - mean * mean
        prm[0, pl.ds(0, n_cb), :] = mean
        prm[1, pl.ds(0, n_cb), :] = lax.rsqrt(var + EPS)
        for cb in range(n_cb):
            cl = pl.ds(cb * LANES, LANES)
            prm[2, pl.ds(cb, 1), :] = bn[pl.ds(0, 1), cl]
            prm[3, pl.ds(cb, 1), :] = bn[pl.ds(1, 1), cl]

    def fill_row(y, s, src, n_cb, pitch, n_col):
        for cb in range(n_cb):
            y[s, cb, :, pl.ds(SUB, n_col), :] = norm(src[cb], cb).reshape(imgs, n_col, LANES)

    def fill_col(y, side, s, cr, n_cb, pitch, n_col, plain):
        at = SUB - 1 if side == 0 else SUB + n_col
        for cb in range(n_cb):
            v = cr[side, s, cb]
            lines(y)[s, cb, pl.ds(at, imgs, stride=pitch), :] = v if plain else norm(v, cb)

    def fill_side_cols(y, set_, z, row, cs, cr, n_rows, n_cb, pitch, n_col, plain):
        for k in (2, 3):
            @pl.when(got(k))
            def _():
                halo_copy(k, set_, z, row, cs, cr, n_rows).wait_recv()
                for s in range(1, n_rows + 1):
                    fill_col(y, 1 if k == 2 else 0, s, cr, n_cb, pitch, n_col, plain)

    def fill_halo_row(y, below, set_, z, row, cs, cr, n_rows, n_cb, pitch, n_col, first):
        args = (set_, z, row, cs, cr, n_rows)
        k = 0 if below else 1
        s = n_rows + 1 if below else 0

        @pl.when(got(k))
        def _():
            if first:
                xrow_copy(k).wait_recv()
                fill_x(s, lambda cl: xrow[1 if below else 0, :, :, cl])
            else:
                halo_copy(k, *args).wait_recv()
                fill_row(y, s, row.at[1 if below else 0], n_cb, pitch, n_col)

        for k, side in ((4, 1), (5, 0)) if below else ((6, 1), (7, 0)):
            @pl.when(got(k))
            def _():
                halo_copy(k, *args).wait_recv()
                fill_col(y, side, s, cr, n_cb, pitch, n_col, first)

    def lhs_of(y, r, n_cb, pitch, starts, n_col, row_step, cb0=0, stride=1, slot0=0):
        parts = []
        for dy in range(3):
            for dx in range(3):
                for cb in range(cb0, cb0 + n_cb):
                    idx = pl.ds(starts + dx, n_col) if stride == 1 else pl.ds(starts + dx, n_col, stride=stride)
                    v = y[row_step * r + slot0 + dy, cb, :, idx, :]
                    parts.append(v.reshape(imgs * n_col, LANES).astype(BF16))
        return jnp.concatenate(parts, axis=1)

    def weights(slot):
        return wsl[slot].reshape(9 * chan, chan)

    def dot(a, b):
        return jnp.dot(a, b, preferred_element_type=F32)

    def add_stats(v, lane0):
        cl = pl.ds(lane0, v.shape[1])
        v3 = v.reshape(v.shape[0] // SUB, SUB, v.shape[1])
        acc[0, :, cl] += jnp.sum(v3, axis=0)
        acc[1, :, cl] += jnp.sum(v3 * v3, axis=0)

    def stat_copy(st, q, p):
        return pltpu.make_async_remote_copy(src_ref=st.at[me], dst_ref=st.at[me], send_sem=ss.at[q], recv_sem=sr.at[q],
                                            device_id=peer(p), device_id_type=MESH)

    def send_stats(st, q, n_cb):
        for m in range(2):
            tot = jnp.sum(acc[m, :, pl.ds(0, n_cb * LANES)], axis=0, keepdims=True)
            for cb in range(n_cb):
                st[me, pl.ds(m * n_cb + cb, 1), :] = tot[:, cb * LANES:(cb + 1) * LANES]

        def go(p, c):
            stat_copy(st, q, p).start()
            return c

        lax.fori_loop(1, n_dev, go, 0)

    def all_of(st, sem):
        part = st.at[pl.ds(0, n_dev - 1)]
        return pltpu.make_async_copy(part, part, sem)

    def clear_stats():
        acc[...] = jnp.zeros_like(acc)

    def mm_row_a(slot, r):
        v = dot(lhs_of(ya, r, cba, pa, SUB - 1, cols, 1), weights(slot))
        add_stats(v, 0)
        for cb in range(cba):
            za[r, cb] = v[:, cb * LANES:(cb + 1) * LANES]

    def layer_a(l, first):
        par = lax.rem(l, 2)
        prev = 1 if first else 1 - par
        args_in = (prev, za, rowa.at[prev], csa, cra.at[prev], rows)
        args_out = (par, za, rowa.at[par], csa, cra.at[par], rows)
        clear_stats()
        if not first:
            def own(r, c):
                fill_row(ya, r + 1, za.at[r], cba, pa, cols)
                return c

            lax.fori_loop(0, rows, own, 0)
        fill_side_cols(ya, *args_in, cba, pa, cols, first)
        wa_copy(l).wait()

        def interior(r, c):
            mm_row_a(l, r)
            return c

        lax.fori_loop(1, rows - 1, interior, 0)

        for k in (0, 1):
            if first:
                @pl.when(here(*KINDS[k]))
                def _():
                    xrow_copy(k).wait_send()
            else:
                halo_sent(k, *args_in)
        for k in range(2, 8):
            halo_sent(k, *args_in)

        for below in (True, False):
            fill_halo_row(ya, below, *args_in, cba, pa, cols, first)

        def edge(t, c):
            mm_row_a(l, jnp.where(t == 0, row_loc, row_rem))
            return c

        lax.fori_loop(0, 2, edge, 0)
        if not first:
            all_of(sta.at[1 - par], ss.at[1 - par]).wait()
        send_stats(sta.at[par], par, cba)
        for side in range(2):
            for r in range(rows):
                for cb in range(cba):
                    csa[side, r, cb] = za[r, cb, pl.ds(side * (cols - 1), imgs, stride=cols), :]
        for k in range(8):
            halo_start(k, *args_out)
        all_of(sta.at[par], sr.at[par]).wait()
        params(sta.at[par], float(n_i * n_j * rows * ma), bna_ref.at[l], cba)

    layer_a(0, True)
    wb_copy(0).start()

    def more(l, c):
        layer_a(l, False)
        return c

    lax.fori_loop(1, layers_a, more, 0)
    for q in range(1, 4):
        wb_copy(q).start()

    last = (layers_a - 1) % 2
    args_in = (last, za, rowa.at[last], csa, cra.at[last], rows)
    args_out = (2, zd, rowb, csb, crb, rowsb)
    clear_stats()

    def own_d(r, c):
        fill_row(ya, r + 1, za.at[r], cba, pa, cols)
        return c

    lax.fori_loop(0, rows, own_d, 0)
    fill_side_cols(ya, *args_in, cba, pa, cols, False)
    for below in (True, False):
        fill_halo_row(ya, below, *args_in, cba, pa, cols, False)
    for k in range(8):
        halo_sent(k, *args_in)
    all_of(sta.at[last], ss.at[last]).wait()
    for nh in range(2):
        wd_copy(nh).wait()

    def down(nh, c):
        a = jnp.concatenate([lhs_of(ya, r, cba, pa, SUB, colb, 2, stride=2, slot0=1) for r in range(rowsb)], axis=0)
        v = dot(a, weights(layers_a + nh))
        v3 = v.reshape(v.shape[0] // SUB, SUB, chan)
        cl = pl.ds(pl.multiple_of(nh * chan, chan), chan)
        acc[0, :, cl] += jnp.sum(v3, axis=0)
        acc[1, :, cl] += jnp.sum(v3 * v3, axis=0)
        for r in range(rowsb):
            for cb in range(cba):
                zd[r, nh * cba + cb] = v[r * mb:(r + 1) * mb, cb * LANES:(cb + 1) * LANES]
        return c

    lax.fori_loop(0, 2, down, 0)
    send_stats(std, 2, cbb)
    for side in range(2):
        for r in range(rowsb):
            for cb in range(cbb):
                csb[side, r, cb] = zd[r, cb, pl.ds(side * (colb - 1), imgs, stride=colb), :]
    for k in range(8):
        halo_start(k, *args_out)
    all_of(std, sr.at[2]).wait()
    n_pos_b = float(n_i * n_j * rowsb * mb)
    params(std, n_pos_b, bnd_ref, cbb)

    clear_stats()

    def own_b(r, c):
        fill_row(yb, r + 1, zd.at[r], cbb, pb, colb)
        return c

    lax.fori_loop(0, rowsb, own_b, 0)
    fill_side_cols(yb, *args_out, cbb, pb, colb, False)
    for below in (True, False):
        fill_halo_row(yb, below, *args_out, cbb, pb, colb, False)
    for q in range(4):
        wb_copy(q).wait()

    def last_mm(nh, c):
        v = None
        for kh in range(2):
            a = jnp.concatenate([lhs_of(yb, r, cba, pb, SUB - 1, colb, 1, cb0=kh * cba) for r in range(rowsb)], axis=0)
            t = dot(a, weights(2 * kh + nh))
            v = t if v is None else v + t
        v3 = v.reshape(v.shape[0] // SUB, SUB, chan)
        cl = pl.ds(pl.multiple_of(nh * chan, chan), chan)
        acc[0, :, cl] += jnp.sum(v3, axis=0)
        acc[1, :, cl] += jnp.sum(v3 * v3, axis=0)
        for r in range(rowsb):
            for cb in range(cba):
                zb[r, nh * cba + cb] = v[r * mb:(r + 1) * mb, cb * LANES:(cb + 1) * LANES]
        return c

    lax.fori_loop(0, 2, last_mm, 0)
    send_stats(stb, 3, cbb)
    for k in range(8):
        halo_sent(k, *args_out)
    all_of(std, ss.at[2]).wait()
    all_of(stb, sr.at[3]).wait()
    params(stb, n_pos_b, bnb_ref.at[0], cbb)

    for r in range(rowsb):
        def fin(g, c):
            at = pl.multiple_of(g * colb, SUB)
            for cb in range(cbb):
                out_ref[g, r, :, pl.ds(cb * LANES, LANES)] = norm(zb[r, cb, pl.ds(at, colb), :], cb).astype(BF16)
            return c

        lax.fori_loop(0, imgs, fin, 0)
    all_of(stb, ss.at[3]).wait()


def solution(mesh):
    n_i, n_j = mesh.shape["sp"], mesh.shape["sp2"]
    n_dev = n_i * n_j

    def per_device(x, w_a, bn_a, w_down, bn_down, w_b, bn_b):
        imgs, rows, cols, chan = x.shape
        chan_b = w_down.shape[-1]
        layers_a = w_a.shape[0]
        cba, cbb = chan // LANES, chan_b // LANES
        colb, rowsb = cols // 2, rows // 2
        ma, mb = imgs * cols, imgs * colb
        pa, pb = cols + 2 * SUB, colb + 2 * SUB
        assert imgs == SUB and layers_a == 4 and w_b.shape[0] == 1 and chan_b == 2 * chan
        dma = pltpu.SemaphoreType.DMA
        hbm = pl.BlockSpec(memory_space=pltpu.HBM)
        vm = pl.BlockSpec(memory_space=pltpu.VMEM)
        scratch = [
            pltpu.VMEM((6, 3, 3, chan, chan), BF16),
            pltpu.VMEM((imgs, rows, cols, chan), BF16),
            pltpu.VMEM((2, imgs, cols, chan), BF16),
            pltpu.VMEM((rows + 2, cba, imgs, pa, LANES), F32),
            pltpu.VMEM((rowsb + 2, cbb, imgs, pb, LANES), F32),
            pltpu.VMEM((rows, cba, ma, LANES), F32),
            pltpu.VMEM((rowsb, cbb, mb, LANES), F32),
            pltpu.VMEM((rowsb, cbb, mb, LANES), F32),
            pltpu.VMEM((2, 2, cba, ma, LANES), F32),
            pltpu.VMEM((2, cbb, mb, LANES), F32),
            pltpu.VMEM((2, rows, cba, SUB, LANES), F32),
            pltpu.VMEM((2, 2, rows + 2, cba, SUB, LANES), F32),
            pltpu.VMEM((2, rowsb, cbb, SUB, LANES), F32),
            pltpu.VMEM((2, rowsb + 2, cbb, SUB, LANES), F32),
            pltpu.VMEM((2, n_dev, 2 * cba, LANES), F32),
            pltpu.VMEM((n_dev, 2 * cbb, LANES), F32),
            pltpu.VMEM((n_dev, 2 * cbb, LANES), F32),
            pltpu.VMEM((2, SUB, chan_b), F32),
            pltpu.VMEM((4, cbb, LANES), F32),
            dma((layers_a + 6,)), dma, dma((2,)), dma((2,)), dma((3, 8)), dma((3, 8)), dma((4,)), dma((4,)),
        ]
        pix = imgs * rows * cols
        flops = 2 * 9 * pix * chan * chan * layers_a + 2 * 9 * (pix // 4) * chan_b * (chan + chan_b)
        return pl.pallas_call(
            functools.partial(stack_kernel, (n_i, n_j, imgs, rows, cols, chan)),
            out_shape=jax.ShapeDtypeStruct((imgs, rowsb, colb, chan_b), BF16),
            in_specs=[hbm, hbm, vm, hbm, vm, hbm, vm],
            out_specs=vm,
            scratch_shapes=scratch,
            cost_estimate=pl.CostEstimate(flops=flops, bytes_accessed=2 * (w_a.size + w_down.size + w_b.size + x.size), transcendentals=0),
            compiler_params=pltpu.CompilerParams(collective_id=0, has_side_effects=True, vmem_limit_bytes=66_000_000),
            name="conv_stack",
        )(x, w_a, bn_a, w_down, bn_down, w_b, bn_b)

    spec = P("dp", "sp", "sp2", None)
    return jax.shard_map(per_device, mesh=mesh, in_specs=(spec, P(), P(), P(), P(), P(), P()), out_specs=spec, check_vma=False)
```

time: 463 us -> 125 us (0.27); the launches traced: 454 us -> 125 us
  blocking collectives: 269 us -> 0 us
  Pallas kernels: 0 us -> 123 us
  matrix products: 66.4 us -> 0 us
  waiting for transfers between devices: 61.8 us -> 0 us
  starting transfers between devices: 48.3 us -> 0 us
    psum x6 -> x0, blocking collectives: 269 us -> none  [conv_bn(): moments = lax.psum(moments, ('sp2', 'sp'))]
    pallas_call x0 -> x1, Pallas kernels: none -> 123 us  [per_device(): pl.pallas_call(functools.partial(stack_kernel, (n_i, n_j, imgs, rows, col...]
    conv_general_dilated x6 -> x0, matrix products: 66.4 us -> none  [conv_bn(): lax.conv_general_dilated(extended, weight, (stride, stride), 'VALID', dim...]
    ppermute x22 -> x0, waiting for transfers between devices: 61.8 us -> none  [the longest x12 49.2 us: edge_extend(): lax.ppermute(first_line, axis_name, perm=[(device + 1, device) for device...]
    ppermute x22 -> x0, starting transfers between devices: 48.3 us -> none  [the longest x10 26.9 us: edge_extend(): lax.ppermute(last_line, axis_name, perm=[(device, device + 1) for device...]
  transfers between devices with their start and end apart: 22 -> 0, of which waited for: 17 -> 0; matrix products, arithmetic and copies ran while one was open for 0% -> 0% of each run, Pallas kernels for 0% -> 0%
where the time goes in v1:
time: 125 us
  Pallas kernels  123 us (98%)
  local copies, waits for them, and re-layouts  2.08 us (2%)
    pallas_call x1, Pallas kernels, per_device(): pl.pallas_call(functools.partial(stack_kernel, (n_i, n_j, imgs, rows, col...  123 us

profile of v1, /device:TPU:97, one launch (start us, length us, event | category | flops | bytes accessed | tf_op | source)
XLA Modules:
  0.0 125.3 jit_solution(2811170545032169271)
XLA Ops:
  0.0 123.2 %conv_stack.1 = bf16[8,2,24,1024]{3,2,1,0:T(8,128)(2,1)} custom-call(bf16[8,4,48,512]{3,2,1,0:T(8,128)(2,1)} %x_hbm.1, bf16[4,3,3,512,512]{4,3,2,1,0:T(8,128)(2,1)} %wa_hbm.1, f32[4,2,512]{2,1,0:T(2,128)} %bna_ref.1, bf16[3,3,512,1024]{3,2,1,0:T(8,128)(2,1)} %wd_hbm.1, f32[2,1024]{1,0:T(2,128)} %bnd_ref.1, bf16[1,3,3,1024,1024]{4,3,2,1,0:T(8,128)(2,1)} %wb_hbm.1, ...), custom_call_target="tpu_custom_call" | custom-call | flops 39862665216 | bytes 48758784 | tf_op jit(solution)/shard_map/conv_stack/pallas_call | solution.py:444
  123.2 2.1 %copy.9 = bf16[8,2,24,1024]{3,2,1,0:T(8,128)(2,1)} copy(bf16[8,2,24,1024]{3,2,1,0:T(8,128)(2,1)} %conv_stack.1) | data formatting | bytes 1572864

commit v2 on v0

v2 whole, which is shorter than its diff:
```python
import functools

import jax
import jax.numpy as jnp
from jax import lax
from jax.experimental import pallas as pl
from jax.experimental.pallas import tpu as pltpu
from jax.sharding import PartitionSpec as P

MESH = pl.DeviceIdType.MESH
F32 = jnp.float32
BF16 = jnp.bfloat16
LANES = 128
SUB = 8
EPS = 1e-5
KINDS = ((-1, 0), (1, 0), (0, -1), (0, 1), (-1, -1), (-1, 1), (1, -1), (1, 1))


def stack_kernel(dims, x_hbm, wa_hbm, bna_ref, wd_hbm, bnd_ref, wb_hbm, bnb_ref, out_ref,
                 wsl, xs, xrow, ya, yb, za, zd, zb, rowa, rowb, csa, cra, csb, crb, sta, std, stb, acc, prm,
                 wsem, xsem, xss, xrs, hs, hr, ss, sr):
    n_i, n_j, imgs, rows, cols, chan = dims
    n_dev = n_i * n_j
    half = chan // 2
    nca = half // LANES
    ncb = 2 * nca
    colb, rowsb = cols // 2, rows // 2
    mb = imgs * colb
    ma = imgs * cols
    layers_a = wa_hbm.shape[0]
    i = lax.axis_index("sp")
    j = lax.axis_index("sp2")
    me = i * n_j + j
    core = lax.rem(i, 2)
    chip = i // 2
    n_chip = n_i // 2
    loc_below = core == 0

    moves = [(dx, dc, dy) for dx in range(n_chip) for dc in range(2) for dy in range(n_j)][1:]
    moves.sort(key=lambda t: -(min(t[0], n_chip - t[0]) + min(t[2], n_j - t[2]) + 0.5 * t[1]))
    sp_of = {(dx, dc): lax.rem(chip + dx, n_chip) * 2 + lax.rem(core + dc, 2) for dx in range(n_chip) for dc in range(2)}
    sp2_of = [lax.rem(j + dy, n_j) for dy in range(n_j)]

    def peer(t):
        return {"sp": sp_of[t[0], t[1]], "sp2": sp2_of[t[2]]}

    def here(di, dj):
        a, b = i + di, j + dj
        return (a >= 0) & (a < n_i) & (b >= 0) & (b < n_j)

    def got(k):
        return here(-KINDS[k][0], -KINDS[k][1])

    def target(k):
        return {"sp": i + KINDS[k][0], "sp2": j + KINDS[k][1]}

    def wa_copy(l):
        return pltpu.make_async_copy(wa_hbm.at[l], wsl.at[l], wsem.at[l])

    def wd_copy(nh):
        return pltpu.make_async_copy(wd_hbm.at[:, :, :, pl.ds(nh * chan, chan)], wsl.at[layers_a + nh], wsem.at[layers_a + nh])

    def wb_copy(q):
        at = pl.ds(pl.multiple_of((q // 2) * chan, chan), chan), pl.ds(pl.multiple_of(lax.rem(q, 2) * chan, chan), chan)
        return pltpu.make_async_copy(wb_hbm.at[0, :, :, at[0], at[1]], wsl.at[q], wsem.at[layers_a + 2 + q])

    xcopy = pltpu.make_async_copy(x_hbm, xs, xsem)
    xcopy.start()
    for l in range(layers_a):
        wa_copy(l).start()
    for nh in range(2):
        wd_copy(nh).start()

    barrier = pltpu.get_barrier_semaphore()
    for t in moves:
        pl.semaphore_signal(barrier, inc=1, device_id=peer(t), device_id_type=MESH)

    def wipe(y):
        def go(t, c):
            y[t] = jnp.zeros(y.shape[1:], F32)
            return c

        lax.fori_loop(0, y.shape[0], go, 0)

    wipe(ya)
    xcopy.wait()
    pl.semaphore_wait(barrier, n_dev - 1)

    def halo_copy(k, c, set_, z, row, cs, cr):
        di, dj = KINDS[k]
        n_rows, n_cb = cs.shape[2], cs.shape[3]
        slot = n_rows + 1 if di < 0 else 0
        edge = 0 if di < 0 else n_rows - 1
        side_here, side_there = (0, 1) if dj < 0 else (1, 0)
        if dj == 0:
            src, dst = z.at[edge, pl.ds(c * n_cb, n_cb)], row.at[1 if di < 0 else 0, pl.ds(c * n_cb, n_cb)]
        elif di == 0:
            src, dst = cs.at[c, side_here], cr.at[c, side_there, pl.ds(1, n_rows)]
        else:
            src, dst = cs.at[c, side_here, edge], cr.at[c, side_there, slot]
        return pltpu.make_async_remote_copy(src_ref=src, dst_ref=dst, send_sem=hs.at[set_, c, k], recv_sem=hr.at[set_, c, k],
                                            device_id=target(k), device_id_type=MESH)

    def halo_start(k, c, bufs, live=None):
        @pl.when(here(*KINDS[k]) if live is None else here(*KINDS[k]) & live)
        def _():
            halo_copy(k, c, *bufs).start()

    def halo_sent(k, c, bufs):
        @pl.when(here(*KINDS[k]))
        def _():
            halo_copy(k, c, *bufs).wait_send()

    def stage_cols(z, cs, c, n_col):
        n_cb = cs.shape[3]
        for side in range(2):
            for r in range(cs.shape[2]):
                for b in range(n_cb):
                    cs[c, side, r, b] = z[r, c * n_cb + b, pl.ds(side * (n_col - 1), imgs, stride=n_col), :]

    def xrow_copy(k, c):
        di = KINDS[k][0]
        cl = pl.ds(c * half, half)
        return pltpu.make_async_remote_copy(src_ref=xs.at[:, 0 if di < 0 else rows - 1, :, cl], dst_ref=xrow.at[1 if di < 0 else 0, :, :, cl],
                                            send_sem=xss.at[c, k], recv_sem=xrs.at[c, k], device_id=target(k), device_id_type=MESH)

    for c in range(2):
        for k in (0, 1):
            @pl.when(here(*KINDS[k]))
            def _():
                xrow_copy(k, c).start()

    def lines(y):
        return y.reshape(y.shape[0], y.shape[1], y.shape[2] * y.shape[3], LANES)

    def fill_x(s, piece, blocks):
        for cb in blocks:
            ya[s, cb, :, pl.ds(SUB, cols), :] = piece(pl.ds(cb * LANES, LANES)).astype(F32)

    def own_x(r, carry):
        fill_x(r + 1, lambda cl: xs[:, r, :, cl], range(2 * nca))
        for cb in range(2 * nca):
            for side in range(2):
                csa[cb // nca, side, r, cb % nca] = lines(ya)[r + 1, cb, pl.ds(SUB + side * (cols - 1), imgs, stride=ya.shape[3]), :]
        return carry

    lax.fori_loop(0, rows, own_x, 0)
    for c in range(2):
        for k in range(2, 8):
            halo_start(k, c, (1, za.at[1], rowa.at[1], csa, cra.at[1]))
    wipe(yb)

    def norm(v, cb):
        mean, rs, gain, shift = (prm[q, pl.ds(cb, 1), :] for q in range(4))
        return jnp.maximum(gain * (v - mean) * rs + shift, 0.0)

    def params(st, n_pos, bn, c, n_cb):
        tot = jnp.sum(st[c], axis=0)
        mean = tot[0:n_cb] / n_pos
        var = tot[n_cb:2 * n_cb] / n_pos - mean * mean
        prm[0, pl.ds(c * n_cb, n_cb), :] = mean
        prm[1, pl.ds(c * n_cb, n_cb), :] = lax.rsqrt(var + EPS)
        for cb in range(c * n_cb, (c + 1) * n_cb):
            cl = pl.ds(cb * LANES, LANES)
            prm[2, pl.ds(cb, 1), :] = bn[pl.ds(0, 1), cl]
            prm[3, pl.ds(cb, 1), :] = bn[pl.ds(1, 1), cl]

    def blocks_of(c, n_cb):
        return range(c * n_cb, (c + 1) * n_cb)

    def fill_row(y, s, src, blocks, n_col):
        for cb in blocks:
            y[s, cb, :, pl.ds(SUB, n_col), :] = norm(src[cb], cb).reshape(imgs, n_col, LANES)

    def fill_own(y, z, c, n_cb, n_rows, n_col):
        def go(r, carry):
            fill_row(y, r + 1, z.at[r], blocks_of(c, n_cb), n_col)
            return carry

        lax.fori_loop(0, n_rows, go, 0)

    def fill_col(y, side, s, c, cr, n_col, plain):
        at = SUB - 1 if side == 0 else SUB + n_col
        n_cb = cr.shape[3]
        for b in range(n_cb):
            v = cr[c, side, s, b]
            w = norm(v, c * n_cb + b)
            lines(y)[s, c * n_cb + b, pl.ds(at, imgs, stride=y.shape[3]), :] = w if plain is None else jnp.where(plain, v, w)

    def fill_sides(y, c, bufs, n_col, plain=None, kinds=(2, 3)):
        n_rows = bufs[3].shape[2]
        for k in kinds:
            @pl.when(got(k))
            def _():
                halo_copy(k, c, *bufs).wait_recv()
                for s in range(1, n_rows + 1):
                    fill_col(y, 1 if k == 2 else 0, s, c, bufs[4], n_col, plain)

    def fill_halo_row(y, below, c, bufs, n_col, cond=True, plain=None, corners=(4, 5, 6, 7)):
        k = 0 if below else 1
        n_rows, n_cb = bufs[3].shape[2], bufs[3].shape[3]
        s = n_rows + 1 if below else 0
        blocks = blocks_of(c, n_cb)

        @pl.when(got(k) & cond)
        def _():
            def from_z():
                halo_copy(k, c, *bufs).wait_recv()
                fill_row(y, s, bufs[2].at[1 if below else 0], blocks, n_col)

            if plain is None:
                from_z()
            else:
                @pl.when(plain)
                def _():
                    xrow_copy(k, c).wait_recv()
                    fill_x(s, lambda cl: xrow[1 if below else 0, :, :, cl], blocks)

                pl.when(jnp.logical_not(plain))(from_z)

        for k2, side in ((4, 1), (5, 0)) if below else ((6, 1), (7, 0)):
            if k2 in corners:
                @pl.when(got(k2) & cond)
                def _():
                    halo_copy(k2, c, *bufs).wait_recv()
                    fill_col(y, side, s, c, bufs[4], n_col, plain)

    def fill_halo_of(y, local, c, bufs, n_col, plain=None):
        for below in (True, False):
            fill_halo_row(y, below, c, bufs, n_col, loc_below if below == local else jnp.logical_not(loc_below), plain)

    def lhs_of(y, r, blocks, start, n_col, stride=1):
        parts = []
        for dy in range(3):
            for dx in range(3):
                for cb in blocks:
                    idx = pl.ds(start + dx, n_col) if stride == 1 else pl.ds(start + dx, n_col, stride=stride)
                    parts.append(y[r + dy, cb, :, idx, :].reshape(imgs * n_col, LANES).astype(BF16))
        return jnp.concatenate(parts, axis=1)

    def weights(slot, k0, nk, n0, nn):
        return wsl[slot, :, :, pl.ds(k0, nk), pl.ds(n0, nn)].reshape(9 * nk, nn)

    def dot(a, b):
        return jnp.dot(a, b, preferred_element_type=F32)

    def put_sums(v, u):
        v3 = v.reshape(v.shape[0] // SUB, SUB, v.shape[1])
        cl = pl.ds(0, v.shape[1])
        acc[u, 0, :, cl] = jnp.sum(v3, axis=0)
        acc[u, 1, :, cl] = jnp.sum(v3 * v3, axis=0)

    def send_stats(st, q, c, n_cb, n_u):
        for m in range(2):
            tot = acc[0, m, :, pl.ds(0, n_cb * LANES)]
            for u in range(1, n_u):
                tot = tot + acc[u, m, :, pl.ds(0, n_cb * LANES)]
            tot = jnp.sum(tot, axis=0, keepdims=True)
            for b in range(n_cb):
                st[c, me, pl.ds(m * n_cb + b, 1), :] = tot[:, b * LANES:(b + 1) * LANES]
        for t in moves:
            pltpu.make_async_remote_copy(src_ref=st.at[c, me], dst_ref=st.at[c, me], send_sem=ss.at[q, c], recv_sem=sr.at[q, c],
                                         device_id=peer(t), device_id_type=MESH).start()

    def stats_all(st, c, sem):
        part = st.at[c, pl.ds(0, n_dev - 1)]
        return pltpu.make_async_copy(part, part, sem)

    pair_loc = jnp.where(loc_below, rows // 2, 0)
    pair_rem = rows // 2 - pair_loc
    hrows = rows // 2
    n_pos_a = float(n_i * n_j * rows * ma)
    n_pos_b = float(n_i * n_j * rowsb * mb)

    def pair_lhs(r0, blocks):
        return jnp.concatenate([lhs_of(ya, r0 + t, blocks, SUB - 1, cols) for t in range(hrows)], axis=0)

    def put_z(z, r0, v, cb0, m):
        for t in range(v.shape[0] // m):
            for b in range(v.shape[1] // LANES):
                z[r0 + t, cb0 + b] = v[t * m:(t + 1) * m, b * LANES:(b + 1) * LANES]

    def get_z(z, r0, n_r, cb0, n_cb):
        return jnp.concatenate([jnp.concatenate([z[r0 + t, cb0 + b] for b in range(n_cb)], axis=1) for t in range(n_r)], axis=0)

    def layer_a(l, carry):
        par = lax.rem(l, 2)
        prev = 1 - par
        first = l == 0
        later = l > 0
        live = l < layers_a - 1
        bin_ = (prev, za.at[prev], rowa.at[prev], csa, cra.at[prev])
        bout = (par, za.at[par], rowa.at[par], csa, cra.at[par])
        z = za.at[par]

        def arrive(c):
            @pl.when(later)
            def _():
                stats_all(sta.at[prev], c, sr.at[prev, c]).wait()
                params(sta.at[prev], n_pos_a, bna_ref.at[jnp.maximum(l - 1, 0)], c, nca)
                fill_own(ya, za.at[prev], c, nca, rows, cols)
                stats_all(sta.at[prev], c, ss.at[prev, c]).wait()

            fill_sides(ya, c, bin_, cols, first)

        def leave(c):
            send_stats(sta.at[par], par, c, nca, 2)
            for k in range(8):
                if k < 2:
                    @pl.when(here(*KINDS[k]) & first)
                    def _():
                        xrow_copy(k, c).wait_send()

                    @pl.when(here(*KINDS[k]) & later)
                    def _():
                        halo_copy(k, c, *bin_).wait_send()
                else:
                    halo_sent(k, c, bin_)
            stage_cols(z, csa, c, cols)
            for k in (2, 3, 4, 5, 6, 7, 0, 1):
                halo_start(k, c, bout, None if k in (0, 2, 4) else live)

        arrive(0)
        fill_halo_of(ya, True, 0, bin_, cols, first)
        wa_copy(l).wait()
        put_z(z, pair_loc, dot(pair_lhs(pair_loc, range(nca)), weights(l, 0, half, 0, chan)), 0, ma)
        fill_halo_of(ya, False, 0, bin_, cols, first)
        put_z(z, pair_rem, dot(pair_lhs(pair_rem, range(nca)), weights(l, 0, half, 0, half)), 0, ma)
        arrive(1)
        fill_halo_of(ya, True, 1, bin_, cols, first)

        def second(u, c):
            @pl.when(u == 1)
            def _():
                fill_halo_of(ya, False, 1, bin_, cols, first)

            r0 = jnp.where(u == 0, pair_loc, pair_rem)
            v = dot(pair_lhs(r0, range(nca, 2 * nca)), weights(l, half, half, 0, half)) + get_z(z, r0, hrows, 0, nca)
            put_sums(v, u)
            put_z(z, r0, v, 0, ma)
            return c

        lax.fori_loop(0, 2, second, 0)
        leave(0)
        v = dot(pair_lhs(pair_rem, range(nca)), weights(l, 0, half, half, half))
        v = v + dot(pair_lhs(pair_rem, range(nca, 2 * nca)), weights(l, half, half, half, half))
        put_sums(v, 0)
        put_z(z, pair_rem, v, nca, ma)
        v = dot(pair_lhs(pair_loc, range(nca, 2 * nca)), weights(l, half, half, half, half)) + get_z(z, pair_loc, hrows, nca, nca)
        put_sums(v, 1)
        put_z(z, pair_loc, v, nca, ma)
        leave(1)
        wb_copy(l).start()
        return carry

    lax.fori_loop(0, layers_a, layer_a, 0)

    last = (layers_a - 1) % 2
    bin_ = (last, za.at[last], rowa.at[last], csa, cra.at[last])
    bmid = (2, zd, rowb, csb, crb)

    def arrive_d(c):
        stats_all(sta.at[last], c, sr.at[last, c]).wait()
        params(sta.at[last], n_pos_a, bna_ref.at[layers_a - 1], c, nca)
        fill_own(ya, za.at[last], c, nca, rows, cols)
        fill_sides(ya, c, bin_, cols, kinds=(2,))
        fill_halo_row(ya, True, c, bin_, cols, corners=(4,))
        stats_all(sta.at[last], c, ss.at[last, c]).wait()
        for k in (0, 2, 4):
            halo_sent(k, c, bin_)

    def leave_d(c):
        send_stats(std, 2, c, ncb, 1)
        stage_cols(zd, csb, c, colb)
        for k in (2, 3, 4, 5, 6, 7, 0, 1):
            halo_start(k, c, bmid)

    def down_lhs(c):
        return jnp.concatenate([lhs_of(ya, 2 * r + 1, blocks_of(c, nca), SUB, colb, 2) for r in range(rowsb)], axis=0)

    arrive_d(0)
    for nh in range(2):
        wd_copy(nh).wait()

    def down0(nh, c):
        v = dot(down_lhs(0), weights(layers_a + nh, 0, half, 0, chan))
        put_z(zd, 0, v, nh * ncb, mb)
        return c

    lax.fori_loop(0, 2, down0, 0)
    arrive_d(1)

    def down1(nh, c):
        v = dot(down_lhs(1), weights(layers_a + nh, half, half, 0, chan)) + get_z(zd, 0, rowsb, nh * ncb, ncb)
        put_sums(v, 0)
        put_z(zd, 0, v, nh * ncb, mb)
        for h in range(2):
            @pl.when(nh == h)
            def _():
                leave_d(h)
        return c

    lax.fori_loop(0, 2, down1, 0)

    def arrive_b(c):
        stats_all(std, c, sr.at[2, c]).wait()
        params(std, n_pos_b, bnd_ref, c, ncb)
        fill_own(yb, zd, c, ncb, rowsb, colb)
        fill_sides(yb, c, bmid, colb)

    row_loc = jnp.where(loc_below, rowsb - 1, 0)

    def row_of(u):
        return jnp.where(u == 0, row_loc, rowsb - 1 - row_loc)

    def b_dot(r, kh, nh):
        return dot(lhs_of(yb, r, blocks_of(kh, ncb), SUB - 1, colb), weights(2 * kh + nh, 0, chan, 0, chan))

    arrive_b(0)
    fill_halo_of(yb, True, 0, bmid, colb)
    for q in range(4):
        wb_copy(q).wait()

    def last0(t, c):
        u, nh = t // 2, lax.rem(t, 2)

        @pl.when(t == 2)
        def _():
            fill_halo_of(yb, False, 0, bmid, colb)

        put_z(zb, row_of(u), b_dot(row_of(u), 0, nh), nh * ncb, mb)
        return c

    lax.fori_loop(0, 4, last0, 0)
    arrive_b(1)
    fill_halo_of(yb, True, 1, bmid, colb)

    def last1(t, c):
        nh, u = t // 2, lax.rem(t, 2)

        @pl.when(t == 1)
        def _():
            fill_halo_of(yb, False, 1, bmid, colb)

        v = b_dot(row_of(u), 1, nh) + get_z(zb, row_of(u), 1, nh * ncb, ncb)
        put_sums(v, u)
        put_z(zb, row_of(u), v, nh * ncb, mb)
        for h in range(2):
            @pl.when(t == 2 * h + 1)
            def _():
                send_stats(stb, 3, h, ncb, 2)
        return c

    lax.fori_loop(0, 4, last1, 0)
    for c in range(2):
        for k in range(8):
            halo_sent(k, c, bmid)
        stats_all(std, c, ss.at[2, c]).wait()

    for c in range(2):
        stats_all(stb, c, sr.at[3, c]).wait()
        params(stb, n_pos_b, bnb_ref.at[0], c, ncb)
        for r in range(rowsb):
            for cb in blocks_of(c, ncb):
                out_ref[:, r, :, pl.ds(cb * LANES, LANES)] = norm(zb[r, cb], cb).reshape(imgs, colb, LANES).astype(BF16)
        stats_all(stb, c, ss.at[3, c]).wait()


def solution(mesh):
    n_i, n_j = mesh.shape["sp"], mesh.shape["sp2"]
    n_dev = n_i * n_j

    def per_device(x, w_a, bn_a, w_down, bn_down, w_b, bn_b):
        imgs, rows, cols, chan = x.shape
        chan_b = w_down.shape[-1]
        layers_a = w_a.shape[0]
        cba, cbb = chan // LANES, chan_b // LANES
        colb, rowsb = cols // 2, rows // 2
        ma, mb = imgs * cols, imgs * colb
        pa, pb = cols + 2 * SUB, colb + 2 * SUB
        assert imgs == SUB and layers_a == 4 and w_b.shape[0] == 1 and chan_b == 2 * chan
        dma = pltpu.SemaphoreType.DMA
        hbm = pl.BlockSpec(memory_space=pltpu.HBM)
        vm = pl.BlockSpec(memory_space=pltpu.VMEM)
        nca, ncb = cba // 2, cbb // 2
        scratch = [
            pltpu.VMEM((layers_a + 2, 3, 3, chan, chan), BF16),
            pltpu.VMEM((imgs, rows, cols, chan), BF16),
            pltpu.VMEM((2, imgs, cols, chan), BF16),
            pltpu.VMEM((rows + 2, cba, imgs, pa, LANES), F32),
            pltpu.VMEM((rowsb + 2, cbb, imgs, pb, LANES), F32),
            pltpu.VMEM((2, rows, cba, ma, LANES), F32),
            pltpu.VMEM((rowsb, cbb, mb, LANES), F32),
            pltpu.VMEM((rowsb, cbb, mb, LANES), F32),
            pltpu.VMEM((2, 2, cba, ma, LANES), F32),
            pltpu.VMEM((2, cbb, mb, LANES), F32),
            pltpu.VMEM((2, 2, rows, nca, SUB, LANES), F32),
            pltpu.VMEM((2, 2, 2, rows + 2, nca, SUB, LANES), F32),
            pltpu.VMEM((2, 2, rowsb, ncb, SUB, LANES), F32),
            pltpu.VMEM((2, 2, rowsb + 2, ncb, SUB, LANES), F32),
            pltpu.VMEM((2, 2, n_dev, 2 * nca, LANES), F32),
            pltpu.VMEM((2, n_dev, 2 * ncb, LANES), F32),
            pltpu.VMEM((2, n_dev, 2 * ncb, LANES), F32),
            pltpu.VMEM((2, 2, SUB, chan), F32),
            pltpu.VMEM((4, cbb, LANES), F32),
            dma((layers_a + 6,)), dma, dma((2, 2)), dma((2, 2)), dma((3, 2, 8)), dma((3, 2, 8)), dma((4, 2)), dma((4, 2)),
        ]
        pix = imgs * rows * cols
        flops = 2 * 9 * pix * chan * chan * layers_a + 2 * 9 * (pix // 4) * chan_b * (chan + chan_b)
        return pl.pallas_call(
            functools.partial(stack_kernel, (n_i, n_j, imgs, rows, cols, chan)),
            out_shape=jax.ShapeDtypeStruct((imgs, rowsb, colb, chan_b), BF16),
            in_specs=[hbm, hbm, vm, hbm, vm, hbm, vm],
            out_specs=vm,
            scratch_shapes=scratch,
            cost_estimate=pl.CostEstimate(flops=flops, bytes_accessed=2 * (w_a.size + w_down.size + w_b.size + x.size), transcendentals=0),
            compiler_params=pltpu.CompilerParams(collective_id=0, has_side_effects=True, vmem_limit_bytes=66_000_000),
            name="conv_stack",
        )(x, w_a, bn_a, w_down, bn_down, w_b, bn_b)

    spec = P("dp", "sp", "sp2", None)
    return jax.shard_map(per_device, mesh=mesh, in_specs=(spec, P(), P(), P(), P(), P(), P()), out_specs=spec, check_vma=False)
```

time: 463 us -> 107 us (0.23); the launches traced: 454 us -> 106 us
  blocking collectives: 269 us -> 0 us
  Pallas kernels: 0 us -> 104 us
  matrix products: 66.4 us -> 0 us
  waiting for transfers between devices: 61.8 us -> 0 us
  starting transfers between devices: 48.3 us -> 0 us
    psum x6 -> x0, blocking collectives: 269 us -> none  [conv_bn(): moments = lax.psum(moments, ('sp2', 'sp'))]
    pallas_call x0 -> x1, Pallas kernels: none -> 104 us  [per_device(): pl.pallas_call(functools.partial(stack_kernel, (n_i, n_j, imgs, rows, col...]
    conv_general_dilated x6 -> x0, matrix products: 66.4 us -> none  [conv_bn(): lax.conv_general_dilated(extended, weight, (stride, stride), 'VALID', dim...]
    ppermute x22 -> x0, waiting for transfers between devices: 61.8 us -> none  [the longest x12 49.2 us: edge_extend(): lax.ppermute(first_line, axis_name, perm=[(device + 1, device) for device...]
    ppermute x22 -> x0, starting transfers between devices: 48.3 us -> none  [the longest x10 26.9 us: edge_extend(): lax.ppermute(last_line, axis_name, perm=[(device, device + 1) for device...]
  transfers between devices with their start and end apart: 22 -> 0, of which waited for: 17 -> 0; matrix products, arithmetic and copies ran while one was open for 0% -> 0% of each run, Pallas kernels for 0% -> 0%
where the time goes in v2:
time: 107 us; the launch traced here: 106 us
  Pallas kernels  104 us (97%)
  local copies, waits for them, and re-layouts  2.08 us (2%)
    pallas_call x1, Pallas kernels, per_device(): pl.pallas_call(functools.partial(stack_kernel, (n_i, n_j, imgs, rows, col...  104 us

profile of v2, /device:TPU:97, one launch (start us, length us, event | category | flops | bytes accessed | tf_op | source)
XLA Modules:
  0.0 106.5 jit_solution(11577502715156024294)
XLA Ops:
  0.0 104.4 %conv_stack.1 = bf16[8,2,24,1024]{3,2,1,0:T(8,128)(2,1)} custom-call(bf16[8,4,48,512]{3,2,1,0:T(8,128)(2,1)} %x_hbm.1, bf16[4,3,3,512,512]{4,3,2,1,0:T(8,128)(2,1)} %wa_hbm.1, f32[4,2,512]{2,1,0:T(2,128)} %bna_ref.1, bf16[3,3,512,1024]{3,2,1,0:T(8,128)(2,1)} %wd_hbm.1, f32[2,1024]{1,0:T(2,128)} %bnd_ref.1, bf16[1,3,3,1024,1024]{4,3,2,1,0:T(8,128)(2,1)} %wb_hbm.1, ...), custom_call_target="tpu_custom_call" | custom-call | flops 39862665216 | bytes 48758784 | tf_op jit(solution)/shard_map/conv_stack/pallas_call | solution.py:510
  104.4 2.1 %copy.9 = bf16[8,2,24,1024]{3,2,1,0:T(8,128)(2,1)} copy(bf16[8,2,24,1024]{3,2,1,0:T(8,128)(2,1)} %conv_stack.1) | data formatting | bytes 1572864

commit v3 on v2

--- a/solution.py
+++ b/solution.py
@@ -66,10 +66,7 @@
 
     xcopy = pltpu.make_async_copy(x_hbm, xs, xsem)
     xcopy.start()
-    for l in range(layers_a):
-        wa_copy(l).start()
-    for nh in range(2):
-        wd_copy(nh).start()
+    wa_copy(0).start()
 
     barrier = pltpu.get_barrier_semaphore()
     for t in moves:
@@ -84,6 +81,10 @@
 
     wipe(ya)
     xcopy.wait()
+    for l in range(1, layers_a):
+        wa_copy(l).start()
+    for nh in range(2):
+        wd_copy(nh).start()
     pl.semaphore_wait(barrier, n_dev - 1)
 
     def halo_copy(k, c, set_, z, row, cs, cr):
@@ -244,11 +245,12 @@
     def dot(a, b):
         return jnp.dot(a, b, preferred_element_type=F32)
 
-    def put_sums(v, u):
+    def put_sums(v, u, more=False):
         v3 = v.reshape(v.shape[0] // SUB, SUB, v.shape[1])
         cl = pl.ds(0, v.shape[1])
-        acc[u, 0, :, cl] = jnp.sum(v3, axis=0)
-        acc[u, 1, :, cl] = jnp.sum(v3 * v3, axis=0)
+        for m, w in enumerate((v3, v3 * v3)):
+            tot = jnp.sum(w, axis=0)
+            acc[u, m, :, cl] = acc[u, m, :, cl] + tot if more else tot
 
     def send_stats(st, q, c, n_cb, n_u):
         for m in range(2):
@@ -272,8 +274,10 @@
     n_pos_a = float(n_i * n_j * rows * ma)
     n_pos_b = float(n_i * n_j * rowsb * mb)
 
-    def pair_lhs(r0, blocks):
-        return jnp.concatenate([lhs_of(ya, r0 + t, blocks, SUB - 1, cols) for t in range(hrows)], axis=0)
+    def pair_dots(l, r0, k, n):
+        w = weights(l, *k, *n)
+        blocks = range(k[0] // LANES, (k[0] + k[1]) // LANES)
+        return [dot(lhs_of(ya, r0 + t, blocks, SUB - 1, cols), w) for t in range(hrows)]
 
     def put_z(z, r0, v, cb0, m):
         for t in range(v.shape[0] // m):
@@ -320,12 +324,25 @@
             for k in (2, 3, 4, 5, 6, 7, 0, 1):
                 halo_start(k, c, bout, None if k in (0, 2, 4) else live)
 
+        lo, hi, full = (0, half), (half, half), (0, chan)
+
+        def finish(u, r0, vs, n):
+            cb0 = n[0] // LANES
+            for t, v in enumerate(vs):
+                put_sums(v, u, t > 0)
+                put_z(z, r0 + t, v, cb0, ma)
+
+        def add_z(vs, r0, n):
+            return [v + get_z(z, r0 + t, 1, n[0] // LANES, nca) for t, v in enumerate(vs)]
+
         arrive(0)
         fill_halo_of(ya, True, 0, bin_, cols, first)
         wa_copy(l).wait()
-        put_z(z, pair_loc, dot(pair_lhs(pair_loc, range(nca)), weights(l, 0, half, 0, chan)), 0, ma)
+        for t, v in enumerate(pair_dots(l, pair_loc, lo, full)):
+            put_z(z, pair_loc + t, v, 0, ma)
         fill_halo_of(ya, False, 0, bin_, cols, first)
-        put_z(z, pair_rem, dot(pair_lhs(pair_rem, range(nca)), weights(l, 0, half, 0, half)), 0, ma)
+        for t, v in enumerate(pair_dots(l, pair_rem, lo, lo)):
+            put_z(z, pair_rem + t, v, 0, ma)
         arrive(1)
         fill_halo_of(ya, True, 1, bin_, cols, first)
 
@@ -335,20 +352,13 @@
                 fill_halo_of(ya, False, 1, bin_, cols, first)
 
             r0 = jnp.where(u == 0, pair_loc, pair_rem)
-            v = dot(pair_lhs(r0, range(nca, 2 * nca)), weights(l, half, half, 0, half)) + get_z(z, r0, hrows, 0, nca)
-            put_sums(v, u)
-            put_z(z, r0, v, 0, ma)
+            finish(u, r0, add_z(pair_dots(l, r0, hi, lo), r0, lo), lo)
             return c
 
         lax.fori_loop(0, 2, second, 0)
         leave(0)
-        v = dot(pair_lhs(pair_rem, range(nca)), weights(l, 0, half, half, half))
-        v = v + dot(pair_lhs(pair_rem, range(nca, 2 * nca)), weights(l, half, half, half, half))
-        put_sums(v, 0)
-        put_z(z, pair_rem, v, nca, ma)
-        v = dot(pair_lhs(pair_loc, range(nca, 2 * nca)), weights(l, half, half, half, half)) + get_z(z, pair_loc, hrows, nca, nca)
-        put_sums(v, 1)
-        put_z(z, pair_loc, v, nca, ma)
+        finish(0, pair_rem, pair_dots(l, pair_rem, full, hi), hi)
+        finish(1, pair_loc, add_z(pair_dots(l, pair_loc, hi, hi), pair_loc, hi), hi)
         leave(1)
         wb_copy(l).start()
         return carry

time: 107 us -> 100 us (0.935)
  Pallas kernels: 104 us -> 97.8 us
    pallas_call x1, Pallas kernels: 104 us -> 97.8 us  [per_device(): pl.pallas_call(functools.partial(stack_kernel, (n_i, n_j, imgs, rows, col...]
where the time goes in v3:
time: 100 us; the launch traced here: 99.9 us
  Pallas kernels  97.8 us (98%)
  local copies, waits for them, and re-layouts  2.08 us (2%)
    pallas_call x1, Pallas kernels, per_device(): pl.pallas_call(functools.partial(stack_kernel, (n_i, n_j, imgs, rows, col...  97.8 us
    unnamed x1, local copies, waits for them, and re-layouts  2.08 us

profile of v3, /device:TPU:97, one launch (start us, length us, event | category | flops | bytes accessed | tf_op | source)
XLA Modules:
  0.0 99.9 jit_solution(13031541384347458245)
XLA Ops:
  0.0 97.8 %conv_stack.1 = bf16[8,2,24,1024]{3,2,1,0:T(8,128)(2,1)} custom-call(bf16[8,4,48,512]{3,2,1,0:T(8,128)(2,1)} %x_hbm.1, bf16[4,3,3,512,512]{4,3,2,1,0:T(8,128)(2,1)} %wa_hbm.1, f32[4,2,512]{2,1,0:T(2,128)} %bna_ref.1, bf16[3,3,512,1024]{3,2,1,0:T(8,128)(2,1)} %wd_hbm.1, f32[2,1024]{1,0:T(2,128)} %bnd_ref.1, bf16[1,3,3,1024,1024]{4,3,2,1,0:T(8,128)(2,1)} %wb_hbm.1, ...), custom_call_target="tpu_custom_call" | custom-call | flops 39862665216 | bytes 48758784 | tf_op jit(solution)/shard_map/conv_stack/pallas_call | solution.py:520
  97.8 2.1 %copy.9 = bf16[8,2,24,1024]{3,2,1,0:T(8,128)(2,1)} copy(bf16[8,2,24,1024]{3,2,1,0:T(8,128)(2,1)} %conv_stack.1) | data formatting | bytes 1572864

commit v4 on v3

--- a/solution.py
+++ b/solution.py
@@ -69,7 +69,7 @@
     wa_copy(0).start()
 
     barrier = pltpu.get_barrier_semaphore()
-    for t in moves:
+    for t in reversed(moves):
         pl.semaphore_signal(barrier, inc=1, device_id=peer(t), device_id_type=MESH)
 
     def wipe(y):
@@ -85,7 +85,6 @@
         wa_copy(l).start()
     for nh in range(2):
         wd_copy(nh).start()
-    pl.semaphore_wait(barrier, n_dev - 1)
 
     def halo_copy(k, c, set_, z, row, cs, cr):
         di, dj = KINDS[k]
@@ -102,6 +101,19 @@
         return pltpu.make_async_remote_copy(src_ref=src, dst_ref=dst, send_sem=hs.at[set_, c, k], recv_sem=hr.at[set_, c, k],
                                             device_id=target(k), device_id_type=MESH)
 
+    def rem_start(c, bufs, pieces, live=True):
+        set_, z, row = bufs[:3]
+        n_rows, n_cb = bufs[3].shape[2], bufs[3].shape[3]
+        m = z.shape[2] // 2
+        for k in (0, 1):
+            @pl.when(here(*KINDS[k]) & (core == k) & (True if k == 0 else live))
+            def _():
+                for p in pieces:
+                    part = lambda ref, at: ref.at[at, c * n_cb + p // 2, pl.ds((p % 2) * m, m)]
+                    pltpu.make_async_remote_copy(src_ref=part(z, 0 if k == 0 else n_rows - 1), dst_ref=part(row, 1 - k),
+                                                 send_sem=hs.at[set_, c, k], recv_sem=hr.at[set_, c, k],
+                                                 device_id=target(k), device_id_type=MESH).start()
+
     def halo_start(k, c, bufs, live=None):
         @pl.when(here(*KINDS[k]) if live is None else here(*KINDS[k]) & live)
         def _():
@@ -125,12 +137,6 @@
         return pltpu.make_async_remote_copy(src_ref=xs.at[:, 0 if di < 0 else rows - 1, :, cl], dst_ref=xrow.at[1 if di < 0 else 0, :, :, cl],
                                             send_sem=xss.at[c, k], recv_sem=xrs.at[c, k], device_id=target(k), device_id_type=MESH)
 
-    for c in range(2):
-        for k in (0, 1):
-            @pl.when(here(*KINDS[k]))
-            def _():
-                xrow_copy(k, c).start()
-
     def lines(y):
         return y.reshape(y.shape[0], y.shape[1], y.shape[2] * y.shape[3], LANES)
 
@@ -146,25 +152,32 @@
         return carry
 
     lax.fori_loop(0, rows, own_x, 0)
+    pl.semaphore_wait(barrier, n_dev - 1)
     for c in range(2):
         for k in range(2, 8):
             halo_start(k, c, (1, za.at[1], rowa.at[1], csa, cra.at[1]))
+    for c in range(2):
+        for k in (0, 1):
+            @pl.when(here(*KINDS[k]))
+            def _():
+                xrow_copy(k, c).start()
     wipe(yb)
 
     def norm(v, cb):
-        mean, rs, gain, shift = (prm[q, pl.ds(cb, 1), :] for q in range(4))
-        return jnp.maximum(gain * (v - mean) * rs + shift, 0.0)
+        mean, gain, shift = (prm[q, pl.ds(cb, 1), :] for q in range(3))
+        return jnp.maximum((v - mean) * gain + shift, 0.0)
 
     def params(st, n_pos, bn, c, n_cb):
         tot = jnp.sum(st[c], axis=0)
         mean = tot[0:n_cb] / n_pos
         var = tot[n_cb:2 * n_cb] / n_pos - mean * mean
         prm[0, pl.ds(c * n_cb, n_cb), :] = mean
-        prm[1, pl.ds(c * n_cb, n_cb), :] = lax.rsqrt(var + EPS)
-        for cb in range(c * n_cb, (c + 1) * n_cb):
+        rs = lax.rsqrt(var + EPS)
+        for b in range(n_cb):
+            cb = c * n_cb + b
             cl = pl.ds(cb * LANES, LANES)
-            prm[2, pl.ds(cb, 1), :] = bn[pl.ds(0, 1), cl]
-            prm[3, pl.ds(cb, 1), :] = bn[pl.ds(1, 1), cl]
+            prm[1, pl.ds(cb, 1), :] = bn[pl.ds(0, 1), cl] * rs[b:b + 1]
+            prm[2, pl.ds(cb, 1), :] = bn[pl.ds(1, 1), cl]
 
     def blocks_of(c, n_cb):
         return range(c * n_cb, (c + 1) * n_cb)
@@ -307,7 +320,7 @@
 
             fill_sides(ya, c, bin_, cols, first)
 
-        def leave(c):
+        def leave(c, pieces):
             send_stats(sta.at[par], par, c, nca, 2)
             for k in range(8):
                 if k < 2:
@@ -321,8 +334,11 @@
                 else:
                     halo_sent(k, c, bin_)
             stage_cols(z, csa, c, cols)
-            for k in (2, 3, 4, 5, 6, 7, 0, 1):
-                halo_start(k, c, bout, None if k in (0, 2, 4) else live)
+            for k in range(2, 8):
+                halo_start(k, c, bout, None if k in (2, 4) else live)
+            for k in (0, 1):
+                halo_start(k, c, bout, core != k if k == 0 else (core != k) & live)
+            rem_start(c, bout, pieces, live)
 
         lo, hi, full = (0, half), (half, half), (0, chan)
 
@@ -345,21 +361,24 @@
             put_z(z, pair_rem + t, v, 0, ma)
         arrive(1)
         fill_halo_of(ya, True, 1, bin_, cols, first)
+        fill_halo_of(ya, False, 1, bin_, cols, first)
 
         def second(u, c):
-            @pl.when(u == 1)
-            def _():
-                fill_halo_of(ya, False, 1, bin_, cols, first)
-
-            r0 = jnp.where(u == 0, pair_loc, pair_rem)
+            r0 = jnp.where(u == 0, pair_rem, pair_loc)
             finish(u, r0, add_z(pair_dots(l, r0, hi, lo), r0, lo), lo)
+
+            @pl.when(u == 0)
+            def _():
+                rem_start(0, bout, range(2), live)
+
             return c
 
         lax.fori_loop(0, 2, second, 0)
-        leave(0)
+        leave(0, range(2, 4))
         finish(0, pair_rem, pair_dots(l, pair_rem, full, hi), hi)
+        rem_start(1, bout, range(1), live)
         finish(1, pair_loc, add_z(pair_dots(l, pair_loc, hi, hi), pair_loc, hi), hi)
-        leave(1)
+        leave(1, range(1, 4))
         wb_copy(l).start()
         return carry
 
@@ -512,7 +531,7 @@
             pltpu.VMEM((2, n_dev, 2 * ncb, LANES), F32),
             pltpu.VMEM((2, n_dev, 2 * ncb, LANES), F32),
             pltpu.VMEM((2, 2, SUB, chan), F32),
-            pltpu.VMEM((4, cbb, LANES), F32),
+            pltpu.VMEM((3, cbb, LANES), F32),
             dma((layers_a + 6,)), dma, dma((2, 2)), dma((2, 2)), dma((3, 2, 8)), dma((3, 2, 8)), dma((4, 2)), dma((4, 2)),
         ]
         pix = imgs * rows * cols

time: 100 us -> 97.6 us (0.976)
  Pallas kernels: 97.8 us -> 95.4 us
    pallas_call x1, Pallas kernels: 97.8 us -> 95.4 us  [per_device(): pl.pallas_call(functools.partial(stack_kernel, (n_i, n_j, imgs, rows, col...]
where the time goes in v4:
time: 97.6 us; the launch traced here: 97.5 us
  Pallas kernels  95.4 us (98%)
  local copies, waits for them, and re-layouts  2.08 us (2%)
    pallas_call x1, Pallas kernels, per_device(): pl.pallas_call(functools.partial(stack_kernel, (n_i, n_j, imgs, rows, col...  95.4 us
    unnamed x1, local copies, waits for them, and re-layouts  2.08 us

profile of v4, /device:TPU:97, one launch (start us, length us, event | category | flops | bytes accessed | tf_op | source)
XLA Modules:
  0.0 97.5 jit_solution(12845325051909471423)
XLA Ops:
  0.0 95.4 %conv_stack.1 = bf16[8,2,24,1024]{3,2,1,0:T(8,128)(2,1)} custom-call(bf16[8,4,48,512]{3,2,1,0:T(8,128)(2,1)} %x_hbm.1, bf16[4,3,3,512,512]{4,3,2,1,0:T(8,128)(2,1)} %wa_hbm.1, f32[4,2,512]{2,1,0:T(2,128)} %bna_ref.1, bf16[3,3,512,1024]{3,2,1,0:T(8,128)(2,1)} %wd_hbm.1, f32[2,1024]{1,0:T(2,128)} %bnd_ref.1, bf16[1,3,3,1024,1024]{4,3,2,1,0:T(8,128)(2,1)} %wb_hbm.1, ...), custom_call_target="tpu_custom_call" | custom-call | flops 39862665216 | bytes 48758784 | tf_op jit(solution)/shard_map/conv_stack/pallas_call | solution.py:539
  95.4 2.1 %copy.9 = bf16[8,2,24,1024]{3,2,1,0:T(8,128)(2,1)} copy(bf16[8,2,24,1024]{3,2,1,0:T(8,128)(2,1)} %conv_stack.1) | data formatting | bytes 1572864

commit v5 on v4

--- a/solution.py
+++ b/solution.py
@@ -258,18 +258,18 @@
     def dot(a, b):
         return jnp.dot(a, b, preferred_element_type=F32)
 
-    def put_sums(v, u, more=False):
+    def put_sums(v, u, more=False, a=0):
         v3 = v.reshape(v.shape[0] // SUB, SUB, v.shape[1])
         cl = pl.ds(0, v.shape[1])
         for m, w in enumerate((v3, v3 * v3)):
             tot = jnp.sum(w, axis=0)
-            acc[u, m, :, cl] = acc[u, m, :, cl] + tot if more else tot
-
-    def send_stats(st, q, c, n_cb, n_u):
+            acc[a, u, m, :, cl] = acc[a, u, m, :, cl] + tot if more else tot
+
+    def send_stats(st, q, c, n_cb, n_u, a=0):
         for m in range(2):
-            tot = acc[0, m, :, pl.ds(0, n_cb * LANES)]
+            tot = acc[a, 0, m, :, pl.ds(0, n_cb * LANES)]
             for u in range(1, n_u):
-                tot = tot + acc[u, m, :, pl.ds(0, n_cb * LANES)]
+                tot = tot + acc[a, u, m, :, pl.ds(0, n_cb * LANES)]
             tot = jnp.sum(tot, axis=0, keepdims=True)
             for b in range(n_cb):
                 st[c, me, pl.ds(m * n_cb + b, 1), :] = tot[:, b * LANES:(b + 1) * LANES]
@@ -450,37 +450,37 @@
     for q in range(4):
         wb_copy(q).wait()
 
-    def last0(t, c):
-        u, nh = t // 2, lax.rem(t, 2)
-
-        @pl.when(t == 2)
+    def last0(u, c):
+        @pl.when(u == 1)
         def _():
             fill_halo_of(yb, False, 0, bmid, colb)
 
-        put_z(zb, row_of(u), b_dot(row_of(u), 0, nh), nh * ncb, mb)
+        for nh in range(2):
+            put_z(zb, row_of(u), b_dot(row_of(u), 0, nh), nh * ncb, mb)
         return c
 
-    lax.fori_loop(0, 4, last0, 0)
+    lax.fori_loop(0, 2, last0, 0)
     arrive_b(1)
     fill_halo_of(yb, True, 1, bmid, colb)
 
-    def last1(t, c):
-        nh, u = t // 2, lax.rem(t, 2)
-
-        @pl.when(t == 1)
-        def _():
-            fill_halo_of(yb, False, 1, bmid, colb)
-
+    def b_finish(u, nh):
         v = b_dot(row_of(u), 1, nh) + get_z(zb, row_of(u), 1, nh * ncb, ncb)
-        put_sums(v, u)
+        put_sums(v, u, a=nh)
         put_z(zb, row_of(u), v, nh * ncb, mb)
+
+    for nh in range(2):
+        b_finish(0, nh)
+    fill_halo_of(yb, False, 1, bmid, colb)
+
+    def last1(nh, c):
+        b_finish(1, nh)
         for h in range(2):
-            @pl.when(t == 2 * h + 1)
-            def _():
-                send_stats(stb, 3, h, ncb, 2)
+            @pl.when(nh == h)
+            def _():
+                send_stats(stb, 3, h, ncb, 2, h)
         return c
 
-    lax.fori_loop(0, 4, last1, 0)
+    lax.fori_loop(0, 2, last1, 0)
     for c in range(2):
         for k in range(8):
             halo_sent(k, c, bmid)
@@ -530,7 +530,7 @@
             pltpu.VMEM((2, 2, n_dev, 2 * nca, LANES), F32),
             pltpu.VMEM((2, n_dev, 2 * ncb, LANES), F32),
             pltpu.VMEM((2, n_dev, 2 * ncb, LANES), F32),
-            pltpu.VMEM((2, 2, SUB, chan), F32),
+            pltpu.VMEM((2, 2, 2, SUB, chan), F32),
             pltpu.VMEM((3, cbb, LANES), F32),
             dma((layers_a + 6,)), dma, dma((2, 2)), dma((2, 2)), dma((3, 2, 8)), dma((3, 2, 8)), dma((4, 2)), dma((4, 2)),
         ]

time: 97.6 us -> 96.5 us (0.989)
  Pallas kernels: 95.4 us -> 94.2 us
    pallas_call x1, Pallas kernels: 95.4 us -> 94.2 us  [per_device(): pl.pallas_call(functools.partial(stack_kernel, (n_i, n_j, imgs, rows, col...]
where the time goes in v5:
time: 96.5 us; the launch traced here: 96.3 us
  Pallas kernels  94.2 us (98%)
  local copies, waits for them, and re-layouts  2.08 us (2%)
    pallas_call x1, Pallas kernels, per_device(): pl.pallas_call(functools.partial(stack_kernel, (n_i, n_j, imgs, rows, col...  94.2 us
    unnamed x1, local copies, waits for them, and re-layouts  2.08 us

profile of v5, /device:TPU:97, one launch (start us, length us, event | category | flops | bytes accessed | tf_op | source)
XLA Modules:
  0.0 96.3 jit_solution(12285175687194885310)
XLA Ops:
  0.0 94.2 %conv_stack.1 = bf16[8,2,24,1024]{3,2,1,0:T(8,128)(2,1)} custom-call(bf16[8,4,48,512]{3,2,1,0:T(8,128)(2,1)} %x_hbm.1, bf16[4,3,3,512,512]{4,3,2,1,0:T(8,128)(2,1)} %wa_hbm.1, f32[4,2,512]{2,1,0:T(2,128)} %bna_ref.1, bf16[3,3,512,1024]{3,2,1,0:T(8,128)(2,1)} %wd_hbm.1, f32[2,1024]{1,0:T(2,128)} %bnd_ref.1, bf16[1,3,3,1024,1024]{4,3,2,1,0:T(8,128)(2,1)} %wb_hbm.1, ...), custom_call_target="tpu_custom_call" | custom-call | flops 39862665216 | bytes 48758784 | tf_op jit(solution)/shard_map/conv_stack/pallas_call | solution.py:539
  94.3 2.1 %copy.9 = bf16[8,2,24,1024]{3,2,1,0:T(8,128)(2,1)} copy(bf16[8,2,24,1024]{3,2,1,0:T(8,128)(2,1)} %conv_stack.1) | data formatting | bytes 1572864
